TPU v7x, 256 devices: a whole 4x4x8 slice. The times are simulated.
256 devices in a mesh: col: 16 (over x, y_lo, core), row: 16 (over z, y_hi).
Axes of the slice: x: 4, y: 4 (y_hi: 2, y_lo: 2; y = y_hi * 2 + y_lo), z: 8, core: 2. Of those that a mesh axis runs over, the one named last changes fastest.
Arguments:
- visibilities: bfloat16 [2, 16384, 16384], P(None, 'col', 'row'), may hold values from -6 to 6
- col_offsets: int32 [16], P('col'), may hold values from 0 to 15360
- row_offsets: int32 [16], replicated, may hold values from 0 to 15360
- facet_offsets: int32 [16, 2], replicated, may hold values from 0 to 16383
- facet_order: int32 [16], replicated, may hold values from 0 to 15, each once
- vis_counts: int32 [16, 16], P('col', 'row'), may hold values from 512 to 1024
Outputs:
- facet_images: float32 [16, 2, 64, 4096], P('col', None, None, 'row')
- peak: float32 [16], P('col')
Inputs may be any that keep to these rules, and one draw needn't show every extreme that they name: `facet_order`: each slot names a different facet.
All inputs are finite; a program needn't handle non-finite values.
Results may differ from a plain program's by a relative error of at most 0.0078.
Values may be sent and summed in bfloat16 or wider, within the bound.
A program may use at most 128 MiB of HBM per device.

v0:
```python
import math

import jax
import jax.numpy as jnp
from jax import lax
from jax.sharding import PartitionSpec as P

M = 1024
FS = 4096
NG = 16384
FR = 64


TWO_PI = 2.0 * math.pi
BEAM_SLOPE = 0.66


def in_blocks(x, dim, length):
    before, after = (x.shape[:dim], x.shape[dim + 1 :])
    return jnp.moveaxis(x.reshape(*before, length, -1, *after), dim, 0)


def sent_and_summed(x, axis, dim):
    pieces = in_blocks(x, dim, lax.axis_size(axis))
    arrived = lax.all_to_all(pieces, axis, split_axis=0, concat_axis=0, tiled=True)
    return arrived.astype(jnp.float32).sum(axis=0)


def copy_for_each(x, axis):
    copies = jnp.broadcast_to(x, (lax.axis_size(axis), *x.shape))
    return lax.all_to_all(copies, axis, split_axis=0, concat_axis=0, tiled=True)


def over_copies(x, axis):
    return copy_for_each(x, axis).max(axis=0)


def phase_table(first_ids, second_ids, factor):
    product = first_ids[:, None] * second_ids[None, :] % NG
    angles = product.astype(jnp.float32) * (TWO_PI / NG)
    return (
        (jnp.cos(angles) * factor).astype(jnp.bfloat16),
        (jnp.sin(angles) * factor).astype(jnp.bfloat16),
    )


def complex_product(left_real, left_imag, right_real, right_imag):
    left_rows = jnp.concatenate([left_real, left_imag], axis=0)
    right_cols = jnp.concatenate([right_real, right_imag], axis=1)
    product = jnp.dot(left_rows, right_cols, preferred_element_type=jnp.float32)
    product = product.reshape(2, left_real.shape[0], 2, right_real.shape[1])
    real_part = product[0, :, 0] - product[1, :, 1]
    imag_part = product[0, :, 1] + product[1, :, 0]
    return (real_part, imag_part)


def local(visibilities, col_offsets, row_offsets, facet_offsets, facet_order, vis_counts):
    col_count = lax.axis_size("col")
    row_count = lax.axis_size("row")
    col_index = lax.axis_index("col")
    row_index = lax.axis_index("row")
    facets = facet_order.shape[0]
    block_cols = FS // row_count
    slot_pick = (facet_order[:, None] == jnp.arange(facets, dtype=jnp.int32)[None, :]).astype(
        jnp.int32
    )
    slot_offsets = jnp.sum(slot_pick[:, :, None] * facet_offsets[None, :, :], axis=1)
    own_pick = (jnp.arange(facets, dtype=jnp.int32) == col_index).astype(jnp.int32)
    own_facet = jnp.sum(slot_offsets * own_pick[:, None], axis=0)
    row_pick = (jnp.arange(row_count, dtype=jnp.int32) == row_index).astype(jnp.int32)
    row_shift = jnp.sum(row_offsets * row_pick)
    row_ids = jnp.arange(M, dtype=jnp.int32)
    live_rows = row_ids < vis_counts[0, 0]
    masked = jnp.where(live_rows[None, :, None], visibilities, jnp.zeros_like(visibilities))
    grid_u = col_offsets[0] + row_ids
    pixel_rows = jnp.arange(FR, dtype=jnp.int32) + (FS // 2 - FR // 2)
    first_scale = 1.0 / math.sqrt(M * col_count)
    second_scale = 0.5 / math.sqrt(M * row_count)
    chosen = slot_offsets[:, 0]
    image_rows = ((chosen[:, None] + pixel_rows[None, :]) % NG).reshape(
        1 * lax.axis_size("col") * FR
    )
    table_real, table_imag = phase_table(image_rows, grid_u, first_scale)
    part_real, part_imag = complex_product(table_real, table_imag, masked[0], masked[1])
    facet_partial = sent_and_summed(
        jnp.stack(
            [
                part_real.reshape(1 * lax.axis_size("col"), FR, M),
                part_imag.reshape(1 * lax.axis_size("col"), FR, M),
            ],
            axis=1,
        ).astype(jnp.bfloat16),
        "col",
        0,
    )[0]
    columns = facet_partial.astype(jnp.bfloat16)
    grid_v = row_shift + row_ids
    image_cols = (
        own_facet[1] + jnp.arange(1 * lax.axis_size("row") * block_cols, dtype=jnp.int32)
    ) % NG
    second_real, second_imag = phase_table(grid_v, image_cols, second_scale)
    out_real, out_imag = complex_product(columns[0], columns[1], second_real, second_imag)
    stacked = jnp.stack([out_real, out_imag], axis=0).reshape(
        2, FR, 1 * lax.axis_size("row"), block_cols
    )
    facet_block = sent_and_summed(
        jnp.transpose(stacked, (2, 0, 1, 3)).astype(jnp.bfloat16), "row", 0
    )[0]
    beam_cols = (row_index * block_cols + jnp.arange(block_cols, dtype=jnp.int32)).astype(
        jnp.float32
    )
    beam = 1.0 - BEAM_SLOPE * (beam_cols + 0.5) / FS
    facet_images = facet_block / beam[None, None, :]
    magnitude = jnp.sqrt(facet_images[0] * facet_images[0] + facet_images[1] * facet_images[1])
    local_peak = jnp.max(magnitude)
    peak = over_copies(local_peak[None], "row")
    return (facet_images[None], peak)


def solution(mesh):
    in_specs = (P(None, "col", "row"), P("col"), P(), P(), P(), P("col", "row"))
    out_specs = (P("col", None, None, "row"), P("col"))
    return jax.shard_map(local, mesh=mesh, in_specs=in_specs, out_specs=out_specs, check_vma=False)
```

profile of v0, /device:TPU:8, one launch (start us, length us, event | category | flops | bytes accessed | tf_op | source)
XLA Modules:
  0.0 257.4 jit_solution(13235904682673704050)
XLA Ops:
  0.6 0.7 fusion.31
  1.4 0.8 multiply_reduce_fusion
  3.6 2.5 broadcast_select_fusion
  6.2 0.4 slice_bitcast_fusion.1
  6.6 17.6 %multiply_convert_fusion.3 = (bf16[1024,1024]{1,0:T(8,128)(2,1)S(1)}, bf16[1024,1024]{1,0:T(8,128)(2,1)S(1)}) fusion(s32[1024]{0:T(1024)S(1)} %get-tuple-element.19, s32[1024]{0:T(1024)S(1)} %get-tuple-element.18), kind=kLoop, calls=%fused_computation.35 | loop fusion | flops 18874368 | bytes 4202496 | tf_op jit(solution)/shard_map/convert_element_type | solution.py:42
  24.2 13.7 %fusion.10 = f32[2048,2048]{1,0:T(8,128)} fusion(bf16[1024,1024]{1,0:T(8,128)(2,1)S(1)} %get-tuple-element.17, bf16[1024,1024]{1,0:T(8,128)(2,1)S(1)} %get-tuple-element.16, bf16[1024,1024]{1,0:T(8,128)(2,1)S(1)} %get-tuple-element.11, bf16[1024,1024]{1,0:T(8,128)(2,1)S(1)} %get-tuple-element.10), kind=kOutput, calls=%fused_computation.22 | convolution fusion | flops 8606711808 | bytes 25165824 | tf_op jit(solution)/shard_map/dot_general | solution.py:50
  37.9 22.0 %reshape.249 = f32[2,1024,2,1024]{3,2,1,0:T(2,128)} reshape(f32[2048,2048]{1,0:T(8,128)} %fusion.10) | data formatting | bytes 33554432 | tf_op jit(solution)/shard_map/reshape | solution.py:51
  60.0 22.7 %fusion.36 = (f32[1,1024,1,1024]{3,2,1,0:T(1,128)S(1)}, f32[1,1024,1,1024]{3,2,1,0:T(1,128)S(1)}, f32[1,1024,1,1024]{3,2,1,0:T(1,128)S(1)}, f32[1,1024,1,1024]{3,2,1,0:T(1,128)S(1)}) fusion(f32[2,1024,2,1024]{3,2,1,0:T(2,128)} %reshape.249), kind=kLoop, calls=%fused_computation.84 | loop fusion | bytes 33554432 | tf_op jit(solution)/shard_map/slice | solution.py:52
  82.7 2.2 fusion.18
  84.9 2.2 fusion.17
  87.5 2.4 copy.43
  89.9 6.6 %all-to-all-start = ((bf16[16,1,2,64,1024]{4,3,2,1,0:T(8,128)(2,1)}), bf16[16,1,2,64,1024]{4,3,2,1,0:T(8,128)(2,1)}, u32[]{:S(2)}, u32[]{:S(2)}) async-start(bf16[16,1,2,64,1024]{4,3,2,1,0:T(8,128)(2,1)} %copy.43), calls=%async_computation | async-start | bytes 8388608 | tf_op jit(solution)/shard_map/all_to_all | solution.py:25
  96.5 0.6 slice.59
  97.1 0.6 fusion.33
  97.8 0.6 iota_add_fusion
  98.4 0.7 add_select_fusion.2
  99.1 69.2 %multiply_convert_fusion.1 = (bf16[1024,4096]{1,0:T(8,128)(2,1)}, bf16[1024,4096]{1,0:T(8,128)(2,1)}) fusion(s32[4096]{0:T(1024)S(1)} %add_select_fusion.2, s32[1024]{0:T(1024)S(1)} %iota_add_fusion), kind=kLoop, calls=%fused_computation.13 | loop fusion | flops 75497472 | bytes 16797696 | tf_op jit(solution)/shard_map/convert_element_type | solution.py:42
  168.3 3.1 %reduce_sum.51 = bf16[2,64,1024]{2,1,0:T(8,128)(2,1)S(1)} reduce(bf16[16,1,2,64,1024]{4,3,2,1,0:T(8,128)(2,1)} %all-to-all-done, bf16[]{:T(256)} %constant.65.clone.1), dimensions={0,1}, to_apply=%region_1.0 | reduce | flops 1966080 | bytes 4456450 | tf_op jit(solution)/shard_map/reduce_sum | solution.py:26
  171.5 9.1 %fusion.3 = f32[128,8192]{1,0:T(8,128)} fusion(bf16[1024,4096]{1,0:T(8,128)(2,1)} %get-tuple-element.15, bf16[1024,4096]{1,0:T(8,128)(2,1)} %get-tuple-element.14, bf16[64,1024]{1,0:T(8,128)(2,1)S(1)} %get-tuple-element.13, bf16[64,1024]{1,0:T(8,128)(2,1)S(1)} %get-tuple-element.12), kind=kOutput, calls=%fused_computation.8 | convolution fusion | flops 2181562368 | bytes 21233664 | tf_op jit(solution)/shard_map/dot_general | solution.py:50
  180.6 6.6 %reshape.250 = f32[2,64,2,4096]{3,2,1,0:T(2,128)} reshape(f32[128,8192]{1,0:T(8,128)} %fusion.3) | data formatting | bytes 8388608 | tf_op jit(solution)/shard_map/reshape | solution.py:51
  187.2 8.9 %fusion.37 = (f32[1,64,1,4096]{3,2,1,0:T(1,128)S(1)}, f32[1,64,1,4096]{3,2,1,0:T(1,128)S(1)}, f32[1,64,1,4096]{3,2,1,0:T(1,128)S(1)}, f32[1,64,1,4096]{3,2,1,0:T(1,128)S(1)}) fusion(f32[2,64,2,4096]{3,2,1,0:T(2,128)} %reshape.250), kind=kLoop, calls=%fused_computation.85 | loop fusion | bytes 8388608 | tf_op jit(solution)/shard_map/slice | solution.py:52
  196.1 1.6 fusion.20
  197.9 1.6 fusion.19
  199.7 1.3 copy.48
  201.1 9.6 %all-to-all-start.1 = ((bf16[16,1,2,64,256]{4,3,2,1,0:T(8,128)(2,1)}), bf16[16,1,2,64,256]{4,3,2,1,0:T(8,128)(2,1)S(1)}, u32[]{:S(2)}, u32[]{:S(2)}) async-start(bf16[16,1,2,64,256]{4,3,2,1,0:T(8,128)(2,1)} %copy.48), calls=%async_computation.1 | async-start | bytes 2097152 | tf_op jit(solution)/shard_map/all_to_all | solution.py:25
  210.7 30.5 %all-to-all-done.1 = bf16[16,1,2,64,256]{4,3,2,1,0:T(8,128)(2,1)S(1)} async-done(((bf16[16,1,2,64,256]{4,3,2,1,0:T(8,128)(2,1)}), bf16[16,1,2,64,256]{4,3,2,1,0:T(8,128)(2,1)S(1)}, u32[]{:S(2)}, u32[]{:S(2)}) %all-to-all-start.1) | async-done | bytes 1048608 | tf_op jit(solution)/shard_map/all_to_all | solution.py:25
  241.4 0.6 fusion.26
  242.0 1.2 broadcast_in_dim.14
  243.3 3.5 %all-to-all-start.2 = ((f32[16,1,1]{2,1,0:T(1,128)}), f32[16,1,1]{2,1,0:T(1,128)S(1)}, u32[]{:S(2)}, u32[]{:S(2)}) async-start(f32[16,1,1]{2,1,0:T(1,128)} %broadcast_in_dim.14), calls=%async_computation.2 | async-start | bytes 16384 | tf_op jit(solution)/shard_map/all_to_all | solution.py:31
  246.8 0.7 bitcast_divide_fusion
  247.5 9.3 %all-to-all-done.2 = f32[16,1,1]{2,1,0:T(1,128)S(1)} async-done(((f32[16,1,1]{2,1,0:T(1,128)}), f32[16,1,1]{2,1,0:T(1,128)S(1)}, u32[]{:S(2)}, u32[]{:S(2)}) %all-to-all-start.2) | async-done | bytes 96 | tf_op jit(solution)/shard_map/all_to_all | solution.py:31
  256.8 0.6 reduce_max.21
  (19 shorter events, 1.2 us)
Async XLA Ops:
  89.9 7.3 %copy-start = (s32[16]{0:T(128)S(1)}, s32[16]{0:T(128)}, u32[]{:S(2)}) copy-start(s32[16]{0:T(128)} %param.8) | copy-start | bytes 196
  89.9 78.5 %all-to-all-start = ((bf16[16,1,2,64,1024]{4,3,2,1,0:T(8,128)(2,1)}), bf16[16,1,2,64,1024]{4,3,2,1,0:T(8,128)(2,1)}, u32[]{:S(2)}, u32[]{:S(2)}) async-start(bf16[16,1,2,64,1024]{4,3,2,1,0:T(8,128)(2,1)} %copy.43), calls=%async_computation | async-start | bytes 8388608 | tf_op jit(solution)/shard_map/all_to_all | solution.py:25
  201.1 40.2 %all-to-all-start.1 = ((bf16[16,1,2,64,256]{4,3,2,1,0:T(8,128)(2,1)}), bf16[16,1,2,64,256]{4,3,2,1,0:T(8,128)(2,1)S(1)}, u32[]{:S(2)}, u32[]{:S(2)}) async-start(bf16[16,1,2,64,256]{4,3,2,1,0:T(8,128)(2,1)} %copy.48), calls=%async_computation.1 | async-start | bytes 2097152 | tf_op jit(solution)/shard_map/all_to_all | solution.py:25
  243.3 13.5 %all-to-all-start.2 = ((f32[16,1,1]{2,1,0:T(1,128)}), f32[16,1,1]{2,1,0:T(1,128)S(1)}, u32[]{:S(2)}, u32[]{:S(2)}) async-start(f32[16,1,1]{2,1,0:T(1,128)} %broadcast_in_dim.14), calls=%async_computation.2 | async-start | bytes 16384 | tf_op jit(solution)/shard_map/all_to_all | solution.py:31
where the time goes:
time: 259 us; the launch traced here: 257 us
  other arithmetic  106 us (41%)
  local copies, waits for them, and re-layouts  66.6 us (26%)
  waiting for transfers between devices  39.8 us (15%)
  matrix products  22.8 us (9%)
  starting transfers between devices  19.7 us (8%)
    convert_element_type x2, other arithmetic, phase_table(): (jnp.cos(angles) * factor).astype(jnp.bfloat16)  86.8 us
    slice x2, local copies, waits for them, and re-layouts, complex_product(): real_part = product[0, :, 0] - product[1, :, 1]  31.7 us
    all_to_all x2, waiting for transfers between devices, sent_and_summed(): lax.all_to_all(pieces, axis, split_axis=0, concat_axis=0, tiled=True)  30.5 us
    reshape x2, local copies, waits for them, and re-layouts, complex_product(): product = product.reshape(2, left_real.shape[0], 2, right_real.shape[1])  28.6 us
    dot_general x2, matrix products, complex_product(): product = jnp.dot(left_rows, right_cols, preferred_element_type=jnp.float32)  22.8 us
    all_to_all x2, starting transfers between devices, sent_and_summed(): lax.all_to_all(pieces, axis, split_axis=0, concat_axis=0, tiled=True)  16.2 us
    all_to_all x1, waiting for transfers between devices, copy_for_each(): return lax.all_to_all(copies, axis, split_axis=0, concat_axis=0, tiled=True)  9.3 us
    another operation x4, other arithmetic  7.63 us
  transfers between devices with their start and end apart: 3, of which 2 were waited for; matrix products, arithmetic and copies ran while one was open for 28% of the time, Pallas kernels for 0%

commit v1 on v0

v1 whole, which is shorter than its diff:
```python
import math

import jax
import jax.numpy as jnp
from jax import lax
from jax.sharding import PartitionSpec as P

M = 1024
FS = 4096
NG = 16384
FR = 64


TWO_PI = 2.0 * math.pi
BEAM_SLOPE = 0.66


def in_blocks(x, dim, length):
    before, after = (x.shape[:dim], x.shape[dim + 1 :])
    return jnp.moveaxis(x.reshape(*before, length, -1, *after), dim, 0)


def sent_and_summed(x, axis):
    arrived = lax.all_to_all(x, axis, split_axis=0, concat_axis=0, tiled=True)
    return arrived.astype(jnp.float32).sum(axis=0)


def wave(first_ids, second_ids, factor=1.0):
    product = first_ids[:, None] * second_ids[None, :] % NG
    angles = product.astype(jnp.float32) * (TWO_PI / NG)
    return jnp.cos(angles) * factor, jnp.sin(angles) * factor


def times(a, b):
    return a[0] * b[0] - a[1] * b[1], a[0] * b[1] + a[1] * b[0]


def local(visibilities, col_offsets, row_offsets, facet_offsets, facet_order, vis_counts):
    col_count = lax.axis_size("col")
    row_count = lax.axis_size("row")
    col_index = lax.axis_index("col")
    row_index = lax.axis_index("row")
    facets = facet_order.shape[0]
    block_cols = FS // row_count
    slot_pick = (facet_order[:, None] == jnp.arange(facets, dtype=jnp.int32)[None, :]).astype(jnp.int32)
    slot_offsets = jnp.sum(slot_pick[:, :, None] * facet_offsets[None, :, :], axis=1)
    own_pick = (jnp.arange(facets, dtype=jnp.int32) == col_index).astype(jnp.int32)
    own_facet = jnp.sum(slot_offsets * own_pick[:, None], axis=0)
    row_pick = (jnp.arange(row_count, dtype=jnp.int32) == row_index).astype(jnp.int32)
    row_shift = jnp.sum(row_offsets * row_pick)
    ids = jnp.arange(M, dtype=jnp.int32)
    live = (ids < vis_counts[0, 0]).astype(jnp.float32)
    first_scale = 1.0 / math.sqrt(M * col_count)
    second_scale = 0.5 / math.sqrt(M * row_count)

    grid_u = col_offsets[0] + ids
    base = wave((slot_offsets[:, 0] + (FS // 2 - FR // 2)) % NG, grid_u, first_scale)
    base = (base[0] * live, base[1] * live)
    steps = wave(jnp.arange(FR, dtype=jnp.int32), grid_u)
    re, im = times((base[0][:, None, :], base[1][:, None, :]), (steps[0][None], steps[1][None]))
    re, im = re.astype(jnp.bfloat16), im.astype(jnp.bfloat16)
    table = jnp.stack([jnp.concatenate([re, -im], axis=-1), jnp.concatenate([im, re], axis=-1)], axis=1)
    part = jnp.dot(
        table.reshape(facets * 2 * FR, 2 * M),
        visibilities.reshape(2 * M, M),
        preferred_element_type=jnp.float32,
    ).astype(jnp.bfloat16)
    columns = sent_and_summed(part.reshape(facets, 2, FR, M), "col")

    grid_v = row_shift + ids
    blocks = jnp.arange(row_count, dtype=jnp.int32)
    twist = wave((own_facet[1] + blocks * block_cols) % NG, grid_v, second_scale)
    fine = wave(grid_v, jnp.arange(block_cols, dtype=jnp.int32))
    fine_re, fine_im = fine[0].astype(jnp.bfloat16), fine[1].astype(jnp.bfloat16)
    right = jnp.concatenate(
        [jnp.concatenate([fine_re, fine_im], axis=1), jnp.concatenate([-fine_im, fine_re], axis=1)], axis=0
    )
    re, im = times((columns[0][None], columns[1][None]), (twist[0][:, None, :], twist[1][:, None, :]))
    left = jnp.concatenate([re, im], axis=-1).astype(jnp.bfloat16).reshape(row_count * FR, 2 * M)
    out = jnp.dot(left, right, preferred_element_type=jnp.float32).astype(jnp.bfloat16)
    facet_block = sent_and_summed(out.reshape(row_count, FR, 2 * block_cols), "row")
    facet_block = jnp.stack([facet_block[:, :block_cols], facet_block[:, block_cols:]])
    beam_cols = (row_index * block_cols + jnp.arange(block_cols, dtype=jnp.int32)).astype(jnp.float32)
    beam = 1.0 - BEAM_SLOPE * (beam_cols + 0.5) / FS
    facet_images = facet_block / beam[None, None, :]
    magnitude = jnp.sqrt(facet_images[0] * facet_images[0] + facet_images[1] * facet_images[1])
    peak = lax.pmax(jnp.max(magnitude)[None], "row")
    return (facet_images[None], peak)


def solution(mesh):
    in_specs = (P(None, "col", "row"), P("col"), P(), P(), P(), P("col", "row"))
    out_specs = (P("col", None, None, "row"), P("col"))
    return jax.shard_map(local, mesh=mesh, in_specs=in_specs, out_specs=out_specs, check_vma=False)
```

time: 259 us -> 184 us (0.71)
  other arithmetic: 106 us -> 31.2 us
  local copies, waits for them, and re-layouts: 66.6 us -> 0.65 us
  blocking collectives: 0 us -> 37.8 us
  waiting for transfers between devices: 39.8 us -> 75.7 us
  matrix products: 22.8 us -> 17.1 us
  starting transfers between devices: 19.7 us -> 16.1 us
    convert_element_type x2, other arithmetic: 86.8 us -> 6.32 us  [the longest x1 5 us: local(): fine[1].astype(jnp.bfloat16)]
    pmax x0 -> x1, blocking collectives: none -> 37.8 us  [local(): peak = lax.pmax(jnp.max(magnitude)[None], 'row')]
    all_to_all x3 -> x2, waiting for transfers between devices: 39.8 us -> 75.7 us  [sent_and_summed(): arrived = lax.all_to_all(x, axis, split_axis=0, concat_axis=0, tiled=True)]
    slice x3 -> x1, local copies, waits for them, and re-layouts: 32.2 us -> 0.59 us  [local(): own_facet[1] + blocks * block_cols]
    reshape x3 -> x0, local copies, waits for them, and re-layouts: 29.9 us -> none  [the longest x2 28.6 us: complex_product(): product = product.reshape(2, left_real.shape[0], 2, right_real.shape[1])]
    dot_general x2, matrix products: 22.8 us -> 17.1 us  [the longest x1 13.8 us: local(): jnp.dot(table.reshape(facets * 2 * FR, 2 * M), visibilities.reshape(2 * M...]
    neg x0 -> x2, other arithmetic: none -> 5.07 us  [the longest x1 4.42 us: local(): -fine_im]
    all_to_all x3 -> x2, starting transfers between devices: 19.7 us -> 16.1 us  [sent_and_summed(): arrived = lax.all_to_all(x, axis, split_axis=0, concat_axis=0, tiled=True)]
  transfers between devices with their start and end apart: 3 -> 2, of which waited for: 2 -> 2; matrix products, arithmetic and copies ran while one was open for 28% -> 7% of each run, Pallas kernels for 0% -> 0%
where the time goes in v1:
time: 184 us; the launch traced here: 181 us
  waiting for transfers between devices  75.7 us (41%)
  blocking collectives  37.8 us (21%)
  other arithmetic  31.2 us (17%)
  matrix products  17.1 us (9%)
  starting transfers between devices  16.1 us (9%)
  between operations  2.07 us (1%)
    all_to_all x2, waiting for transfers between devices, sent_and_summed(): arrived = lax.all_to_all(x, axis, split_axis=0, concat_axis=0, tiled=True)  75.7 us
    pmax x1, blocking collectives, local(): peak = lax.pmax(jnp.max(magnitude)[None], 'row')  37.8 us
    all_to_all x2, starting transfers between devices, sent_and_summed(): arrived = lax.all_to_all(x, axis, split_axis=0, concat_axis=0, tiled=True)  16.1 us
    dot_general x1, matrix products, local(): jnp.dot(table.reshape(facets * 2 * FR, 2 * M), visibilities.reshape(2 * M...  13.8 us
    another operation x2, other arithmetic, local(): jnp.stack([jnp.concatenate([re, -im], axis=-1), jnp.concatenate([im, re],...  8.52 us
    convert_element_type x1, other arithmetic, local(): fine[1].astype(jnp.bfloat16)  5 us
    neg x1, other arithmetic, local(): -fine_im  4.42 us
  transfers between devices with their start and end apart: 2, of which 2 were waited for; matrix products, arithmetic and copies ran while one was open for 7% of the time, Pallas kernels for 0%

profile of v1, /device:TPU:8, one launch (start us, length us, event | category | flops | bytes accessed | tf_op | source)
XLA Modules:
  0.0 180.6 jit_solution(14930321592499214702)
XLA Ops:
  0.6 0.7 fusion.40
  1.4 0.8 multiply_reduce_fusion
  3.5 1.0 fusion.30
  4.5 0.3 cosine_multiply_fusion.1
  4.9 1.3 add_convert_fusion.1
  6.2 0.7 fusion.47
  6.9 2.3 %maximum_bitcast_fusion = (bf16[16,1,64,2048]{3,2,1,0:T(8,128)(2,1)S(1)}, bf16[16,1,64,2048]{3,2,1,0:T(8,128)(2,1)}) fusion(bf16[16,64,1024]{2,1,0:T(8,128)(2,1)S(1)} %fusion.47, bf16[16,64,1024]{2,1,0:T(8,128)(2,1)S(1)} %get-tuple-element.7, bf16[16,64,1024]{2,1,0:T(8,128)(2,1)S(1)} %get-tuple-element.6), kind=kLoop, calls=%fused_computation.2 | loop fusion | flops 16777216 | bytes 14680064 | tf_op jit(solution)/shard_map/stack | solution.py:62
  9.2 6.2 %pad_maximum_fusion = bf16[16,2,64,2048]{3,2,1,0:T(8,128)(2,1)} fusion(bf16[16,1,64,2048]{3,2,1,0:T(8,128)(2,1)} %get-tuple-element.3, bf16[16,1,64,2048]{3,2,1,0:T(8,128)(2,1)S(1)} %get-tuple-element.2), kind=kLoop, calls=%fused_computation | loop fusion | flops 4194304 | bytes 16777216 | tf_op jit(solution)/shard_map/stack | solution.py:62
  15.4 13.8 %convolution_convert_fusion = bf16[2048,1024]{1,0:T(8,128)(2,1)} fusion(bf16[2048,2048]{1,0:T(8,128)(2,1)} %bitcast.34, bf16[2048,1024]{1,0:T(8,128)(2,1)} %bitcast.38), kind=kOutput, calls=%fused_computation.12 | convolution fusion | flops 8592031744 | bytes 16777216 | tf_op jit(solution)/shard_map/dot_general | solution.py:63
  29.1 0.0 copy-start
  29.1 6.6 %all-to-all-start = ((bf16[16,2,64,1024]{3,2,1,0:T(8,128)(2,1)}), bf16[16,2,64,1024]{3,2,1,0:T(8,128)(2,1)}, u32[]{:S(2)}, u32[]{:S(2)}) async-start(bf16[16,2,64,1024]{3,2,1,0:T(8,128)(2,1)} %bitcast.35), calls=%async_computation | async-start | bytes 8388608 | tf_op jit(solution)/shard_map/all_to_all | solution.py:24
  35.7 0.1 multiply_reduce_fusion.1
  35.8 0.6 slice.28
  36.4 0.7 and_select_fusion
  37.1 0.0 copy-done
  37.1 0.6 fusion.43
  37.7 0.6 iota_add_fusion
  38.4 0.3 cosine_multiply_fusion
  38.7 4.4 %fusion.28 = bf16[1024,256]{1,0:T(8,128)(2,1)S(1)} fusion(s32[1024]{0:T(1024)S(1)} %iota_add_fusion), kind=kLoop, calls=%fused_computation.44 | loop fusion | flops 4718592 | bytes 528384 | tf_op jit(solution)/shard_map/neg | solution.py:76
  43.1 5.0 %sine_convert_fusion = (bf16[1024,256]{1,0:T(8,128)(2,1)S(1)}, bf16[1024,256]{1,0:T(8,128)(2,1)S(1)}) fusion(s32[1024]{0:T(1024)S(1)} %iota_add_fusion), kind=kLoop, calls=%fused_computation.28 | loop fusion | flops 4194304 | bytes 1052672 | tf_op jit(solution)/shard_map/convert_element_type | solution.py:74
  48.1 44.9 %all-to-all-done = bf16[16,2,64,1024]{3,2,1,0:T(8,128)(2,1)} async-done(((bf16[16,2,64,1024]{3,2,1,0:T(8,128)(2,1)}), bf16[16,2,64,1024]{3,2,1,0:T(8,128)(2,1)}, u32[]{:S(2)}, u32[]{:S(2)}) %all-to-all-start) | async-done | bytes 4194336 | tf_op jit(solution)/shard_map/all_to_all | solution.py:24
  93.0 3.2 %convert_reduce_fusion = f32[2,64,1024]{2,1,0:T(8,128)S(1)} fusion(bf16[16,2,64,1024]{3,2,1,0:T(8,128)(2,1)} %all-to-all-done), kind=kLoop, calls=%fused_computation.1 | loop fusion | flops 4063232 | bytes 4718592 | tf_op jit(solution)/shard_map/reduce_sum | solution.py:25
  96.2 1.3 subtract_convert_fusion
  97.5 3.3 %fusion.11 = bf16[1024,512]{1,0:T(8,128)(2,1)} fusion(bf16[1024,256]{1,0:T(8,128)(2,1)S(1)} %get-tuple-element.21, bf16[1024,256]{1,0:T(8,128)(2,1)S(1)} %fusion.28, bf16[1024,256]{1,0:T(8,128)(2,1)S(1)} %get-tuple-element.20, bf16[1024,1024]{1,0:T(8,128)(2,1)S(1)} %bitcast.37, bf16[1024,1024]{1,0:T(8,128)(2,1)S(1)} %bitcast.36), kind=kOutput, calls=%fused_computation.24 | convolution fusion | flops 2164785152 | bytes 6815744 | tf_op jit(solution)/shard_map/dot_general | solution.py:80
  100.9 9.5 %all-to-all-start.1 = ((bf16[16,64,512]{2,1,0:T(8,128)(2,1)}), bf16[16,64,512]{2,1,0:T(8,128)(2,1)S(1)}, u32[]{:S(2)}, u32[]{:S(2)}) async-start(bf16[16,64,512]{2,1,0:T(8,128)(2,1)} %bitcast.14), calls=%async_computation.1 | async-start | bytes 2097152 | tf_op jit(solution)/shard_map/all_to_all | solution.py:24
  110.4 30.8 %all-to-all-done.1 = bf16[16,64,512]{2,1,0:T(8,128)(2,1)S(1)} async-done(((bf16[16,64,512]{2,1,0:T(8,128)(2,1)}), bf16[16,64,512]{2,1,0:T(8,128)(2,1)S(1)}, u32[]{:S(2)}, u32[]{:S(2)}) %all-to-all-start.1) | async-done | bytes 1048608 | tf_op jit(solution)/shard_map/all_to_all | solution.py:24
  141.2 0.1 convert_reduce_fusion.1
  141.4 0.6 fusion.39
  142.1 37.8 %pmax.7 = f32[1]{0:T(128)} all-reduce(f32[1]{0:T(128)} %bitcast.19), channel_id=1, replica_groups=mesh['col'=16,'row'=16] {'row'}, use_global_device_ids=true, to_apply=%region_6.7 | all-reduce | flops 1 | bytes 8 | tf_op jit(solution)/shard_map/pmax | solution.py:87
  179.9 0.7 maximum_divide_fusion
  (8 shorter events, 0.1 us)
Async XLA Ops:
  29.1 7.9 %copy-start = (s32[16]{0:T(128)S(1)}, s32[16]{0:T(128)}, u32[]{:S(2)}) copy-start(s32[16]{0:T(128)} %param.8) | copy-start | bytes 196
  29.1 63.9 %all-to-all-start = ((bf16[16,2,64,1024]{3,2,1,0:T(8,128)(2,1)}), bf16[16,2,64,1024]{3,2,1,0:T(8,128)(2,1)}, u32[]{:S(2)}, u32[]{:S(2)}) async-start(bf16[16,2,64,1024]{3,2,1,0:T(8,128)(2,1)} %bitcast.35), calls=%async_computation | async-start | bytes 8388608 | tf_op jit(solution)/shard_map/all_to_all | solution.py:24
  100.9 40.4 %all-to-all-start.1 = ((bf16[16,64,512]{2,1,0:T(8,128)(2,1)}), bf16[16,64,512]{2,1,0:T(8,128)(2,1)S(1)}, u32[]{:S(2)}, u32[]{:S(2)}) async-start(bf16[16,64,512]{2,1,0:T(8,128)(2,1)} %bitcast.14), calls=%async_computation.1 | async-start | bytes 2097152 | tf_op jit(solution)/shard_map/all_to_all | solution.py:24

commit v2 on v1

v2 whole, which is shorter than its diff:
```python
import math

import jax
import jax.numpy as jnp
from jax import lax
from jax.experimental import pallas as pl
from jax.experimental.pallas import tpu as pltpu
from jax.sharding import PartitionSpec as P

MESH = pl.DeviceIdType.MESH
F32, BF16, I32 = jnp.float32, jnp.bfloat16, jnp.int32

M = 1024
FS = 4096
NG = 16384
FR = 64
NF = 16
CH = 16
NCH = FR // CH
JB = FS // NF
TWO_PI = 2.0 * math.pi
BEAM_SLOPE = 0.66
FIRST_SCALE = 1.0 / math.sqrt(NG)
SECOND_SCALE = 0.5 / math.sqrt(NG)

CORE, XA_UP, XB_UP, XA_DN, XB_DN, XC_UP, XC_DN, YLO, YHI, ZUP, ZDN = 0, 1, 2, 3, 4, 5, 6, 7, 8, 9, 13
COPIES = 17


def wave(exponent):
    angle = (exponent & (NG - 1)).astype(F32) * (TWO_PI / NG)
    return jnp.cos(angle), jnp.sin(angle)


def times(a, b):
    return a[0] * b[0] - a[1] * b[1], a[0] * b[1] + a[1] * b[0]


def iota(shape, dim):
    return lax.broadcasted_iota(I32, shape, dim)


def column_of(scalars, shape):
    row = iota(shape, 0)
    picked = jnp.zeros(shape, I32)
    for index, value in enumerate(scalars):
        picked = jnp.where(row == index, value, picked)
    return picked


def body(
    vis, col_offsets, row_offsets, facet_offsets, facet_order, vis_counts,
    out, peak,
    grid, table, unit_re, unit_im, part, part_in, own,
    xa_send, xb_send, xc_send, xa_recv, xb_recv, xc_recv, y_send, y_recv,
    twist_re, twist_im, left, fine, image, z_send, z_recv, h_send, h_recv, top, tops,
    load_sem, send_sem, recv_sem, top_send, top_recv,
):
    c, r = lax.axis_index("col"), lax.axis_index("row")
    x, ylo, core = c // 4, (c // 2) % 2, c % 2
    z, yhi = r // 2, r % 2
    to_core = (c + 1 - 2 * core, r)
    to_ylo = (c + 2 - 4 * ylo, r)
    to_yhi = (c, r + 1 - 2 * yhi)
    x_up, x_dn = ((c + 4) % 16, r), ((c + 12) % 16, r)
    z_up, z_dn = (c, (r + 2) % 16), (c, (r + 14) % 16)

    loads = [pltpu.make_async_copy(vis.at[p], grid.at[p], load_sem.at[p]) for p in range(2)]
    for load in loads:
        load.start()
    barrier = pltpu.get_barrier_semaphore()
    for peer in (to_core, to_ylo, x_up, x_dn):
        pl.semaphore_signal(barrier, inc=1, device_id=peer, device_id_type=MESH)
    for step in range(1, NF):
        pl.semaphore_signal(barrier, inc=1, device_id=(c, (r + step) % NF), device_id_type=MESH)

    started = []

    def send(src, dst, k, index, peer):
        copy = pltpu.make_async_remote_copy(
            src_ref=src, dst_ref=dst, send_sem=send_sem.at[k, index], recv_sem=recv_sem.at[k, index],
            device_id=peer, device_id_type=MESH,
        )
        copy.start()
        started.append(copy)
        return copy

    slots = [
        ((x + dx) % 4) * 4 + ((ylo + dy) % 2) * 2 + (core + 1 - half) % 2
        for half in range(2) for dx in range(4) for dy in range(2)
    ]
    rows_at = [facet_offsets[facet_order[s], 0] + (FS // 2 - FR // 2) for s in slots]
    wide = (NF, M)
    place = iota(wide, 1)
    grid_u = col_offsets[0] + place
    live = (place < vis_counts[0, 0]).astype(F32) * FIRST_SCALE
    slot_rows = column_of(rows_at, wide)
    unit = wave(grid_u * iota(wide, 0))
    unit_re[...], unit_im[...] = unit

    copies = [dict() for _ in range(NCH)]

    def build(k):
        base = wave(grid_u * ((slot_rows + CH * k) & (NG - 1)))
        base = (base[0] * live, base[1] * live)
        for half in range(2):
            for dx in range(4):
                for dy in range(2):
                    s = half * 8 + dx * 2 + dy
                    re, im = times((base[0][s : s + 1], base[1][s : s + 1]), (unit_re[...], unit_im[...]))
                    re, im = re.astype(BF16), im.astype(BF16)
                    table[half, dx, 0, dy, :, :M] = re
                    table[half, dx, 0, dy, :, M:] = -im
                    table[half, dx, 1, dy, :, :M] = im
                    table[half, dx, 1, dy, :, M:] = re

    def multiply(half):
        return jnp.dot(
            table[half].reshape(16 * CH, 2 * M), grid[...].reshape(2 * M, M), preferred_element_type=F32
        ).reshape(4, 2, 2, CH, M)

    def first(k):
        build(k)
        part[k] = multiply(0).astype(BF16)
        if k == 0:
            pl.semaphore_wait(barrier, 4 + NF - 1)
        copies[k]["core"] = send(part.at[k], part_in.at[k], k, CORE, to_core)
        own[k] = multiply(1)

    def spread_x(k):
        copies[k]["core"].wait_recv()
        xa_send[k, 0] = (own[k, 2, 0] + part_in[k, 2, 0].astype(F32)).astype(BF16)
        copies[k]["xa_up"] = send(xa_send.at[k, 0], xa_recv.at[k, 0], k, XA_UP, x_up)
        xa_send[k, 1] = (own[k, 2, 1] + part_in[k, 2, 1].astype(F32)).astype(BF16)
        copies[k]["xa_dn"] = send(xa_send.at[k, 1], xa_recv.at[k, 1], k, XA_DN, x_dn)
        xb_send[k, 0] = (own[k, 1, 1] + part_in[k, 1, 1].astype(F32)).astype(BF16)
        copies[k]["xb_up"] = send(xb_send.at[k, 0], xb_recv.at[k, 0], k, XB_UP, x_up)
        xb_send[k, 1] = (own[k, 3, 0] + part_in[k, 3, 0].astype(F32)).astype(BF16)
        copies[k]["xb_dn"] = send(xb_send.at[k, 1], xb_recv.at[k, 1], k, XB_DN, x_dn)
        own[k, 1, 0] = own[k, 1, 0] + part_in[k, 1, 0].astype(F32)
        own[k, 3, 1] = own[k, 3, 1] + part_in[k, 3, 1].astype(F32)
        own[k, 0] = own[k, 0] + part_in[k, 0].astype(F32)

    def relay_x(k):
        copies[k]["xa_up"].wait_recv()
        xc_send[k, 0] = (own[k, 1, 0] + xa_recv[k, 0].astype(F32)).astype(BF16)
        copies[k]["xc_up"] = send(xc_send.at[k, 0], xc_recv.at[k, 0], k, XC_UP, x_up)
        copies[k]["xa_dn"].wait_recv()
        xc_send[k, 1] = (own[k, 3, 1] + xa_recv[k, 1].astype(F32)).astype(BF16)
        copies[k]["xc_dn"] = send(xc_send.at[k, 1], xc_recv.at[k, 1], k, XC_DN, x_dn)

    def hop_y(k):
        for name in ("xb_up", "xb_dn", "xc_up", "xc_dn"):
            copies[k][name].wait_recv()
        y_send[k, 0] = (own[k, 0, 0, 1] + xb_recv[k, 1, 1].astype(F32) + xc_recv[k, 0, 1].astype(F32)).astype(BF16)
        y_send[k, 1] = (own[k, 0, 1, 1] + xb_recv[k, 0, 1].astype(F32) + xc_recv[k, 1, 1].astype(F32)).astype(BF16)
        copies[k]["y"] = send(y_send.at[k], y_recv.at[k], k, YLO, to_ylo)
        own[k, 0, 0, 0] = own[k, 0, 0, 0] + xb_recv[k, 1, 0].astype(F32) + xc_recv[k, 0, 0].astype(F32)
        own[k, 0, 1, 0] = own[k, 0, 1, 0] + xb_recv[k, 0, 0].astype(F32) + xc_recv[k, 1, 0].astype(F32)

    def prepare():
        grid_v = row_offsets[r] + place
        start = facet_offsets[facet_order[c], 1]
        block = 2 * ((z + iota(wide, 0) // 2) % 8) + (yhi + iota(wide, 0)) % 2
        twist = wave(grid_v * ((start + JB * block) & (NG - 1)))
        twist_re[...] = twist[0] * SECOND_SCALE
        twist_im[...] = twist[1] * SECOND_SCALE
        shape = (32, JB)
        coarse = wave((row_offsets[r] + 32 * iota(shape, 0)) * iota(shape, 1))
        small = wave(iota(shape, 0) * iota(shape, 1))
        for v in range(32):
            re, im = times((coarse[0][v : v + 1], coarse[1][v : v + 1]), small)
            re, im = re.astype(BF16), im.astype(BF16)
            fine[32 * v : 32 * v + 32, :JB] = re
            fine[32 * v : 32 * v + 32, JB:] = im
            fine[M + 32 * v : M + 32 * v + 32, :JB] = -im
            fine[M + 32 * v : M + 32 * v + 32, JB:] = re

    def second(k):
        copies[k]["y"].wait_recv()
        columns = (own[k, 0, 0, 0] + y_recv[k, 0].astype(F32), own[k, 0, 1, 0] + y_recv[k, 1].astype(F32))
        for b in range(NF):
            re, im = times(columns, (twist_re[b : b + 1, :], twist_im[b : b + 1, :]))
            left[b, :, :M] = re.astype(BF16)
            left[b, :, M:] = im.astype(BF16)
        image[k] = jnp.dot(
            left[...].reshape(NF * CH, 2 * M), fine[...], preferred_element_type=F32
        ).reshape(8, 2, CH, 2 * JB)
        z_send[k, 0, 0, :, :, :JB] = image[k, 4, :, :, :JB].astype(BF16)
        z_send[k, 1, 0, :, :, JB:] = image[k, 4, :, :, JB:].astype(BF16)
        copies[k]["up0"] = send(
            z_send.at[k, 0, 0, :, :, pl.ds(0, JB)], z_recv.at[k, 0, 0, :, :, pl.ds(0, JB)], k, ZUP, z_up
        )
        copies[k]["dn0"] = send(
            z_send.at[k, 1, 0, :, :, pl.ds(JB, JB)], z_recv.at[k, 1, 0, :, :, pl.ds(JB, JB)], k, ZDN, z_dn
        )

    def relay_z(k, step):
        for way, name, peer, at, index, half in (
            (0, "up", z_up, 4 - step, ZUP, slice(0, JB)),
            (1, "dn", z_dn, 4 + step, ZDN, slice(JB, 2 * JB)),
        ):
            copies[k][f"{name}{step - 1}"].wait_recv()
            if step == 1:
                other = slice(JB, 2 * JB) if way == 0 else slice(0, JB)
                z_send[k, way, step, :, :, half] = (
                    image[k, at, :, :, half] + z_recv[k, way, 0, :, :, half].astype(F32)
                ).astype(BF16)
                z_send[k, way, step, :, :, other] = image[k, at, :, :, other].astype(BF16)
            else:
                z_send[k, way, step] = (image[k, at] + z_recv[k, way, step - 1].astype(F32)).astype(BF16)
            copies[k][f"{name}{step}"] = send(
                z_send.at[k, way, step], z_recv.at[k, way, step], k, index + step, peer
            )

    def hop_h(k):
        copies[k]["up3"].wait_recv()
        copies[k]["dn3"].wait_recv()
        total = image[k, 0] + z_recv[k, 0, 3].astype(F32) + z_recv[k, 1, 3].astype(F32)
        h_send[k] = total[1].astype(BF16)
        copies[k]["h"] = send(h_send.at[k], h_recv.at[k], k, YHI, to_yhi)
        image[k, 0, 0] = total[0]

    column = (r * JB + iota((CH, JB), 1)).astype(F32)
    beam = 1.0 - BEAM_SLOPE * (column + 0.5) / FS

    def finish(k):
        copies[k]["h"].wait_recv()
        total = image[k, 0, 0] + h_recv[k].astype(F32)
        re, im = total[:, :JB] / beam, total[:, JB:] / beam
        out[0, 0, CH * k : CH * k + CH, :] = re
        out[0, 1, CH * k : CH * k + CH, :] = im
        power = re * re + im * im
        power = jnp.maximum(power[:8], power[8:])
        power = jnp.maximum(power[:, :128], power[:, 128:])
        top[...] = power if k == 0 else jnp.maximum(top[...], power)

    for load in loads:
        load.wait()
    for name, k in ORDER:
        if name == "first":
            first(k)
        elif name == "spread":
            spread_x(k)
        elif name == "relay":
            relay_x(k)
        elif name == "hop_y":
            hop_y(k)
        elif name == "prepare":
            prepare()
        elif name == "second":
            second(k)
        elif name.startswith("z"):
            relay_z(k, int(name[1:]))
        elif name == "hop_h":
            hop_h(k)
        elif name == "finish":
            finish(k)

    top[...] = jnp.sqrt(top[...])
    sends = []
    for step in range(1, NF):
        copy = pltpu.make_async_remote_copy(
            src_ref=top, dst_ref=tops.at[step], send_sem=top_send.at[step], recv_sem=top_recv.at[step],
            device_id=(c, (r + step) % NF), device_id_type=MESH,
        )
        copy.start()
        sends.append(copy)
    best = top[...]
    for step in range(1, NF):
        sends[step - 1].wait_recv()
        best = jnp.maximum(best, tops[step])
    peak[0] = jnp.max(best)
    for copy in started + sends:
        copy.wait_send()


ORDER = (
    ("first", 0), ("spread", 0),
    ("first", 1), ("spread", 1), ("relay", 0),
    ("first", 2), ("spread", 2), ("hop_y", 0), ("relay", 1),
    ("first", 3), ("spread", 3), ("prepare", 0), ("second", 0), ("hop_y", 1), ("relay", 2),
    ("z1", 0), ("second", 1), ("z2", 0), ("hop_y", 2), ("relay", 3), ("z1", 1), ("z3", 0),
    ("second", 2), ("hop_h", 0), ("z2", 1), ("hop_y", 3), ("z1", 2), ("z3", 1), ("finish", 0),
    ("second", 3), ("hop_h", 1), ("z2", 2), ("z1", 3), ("z3", 2), ("finish", 1), ("z2", 3), ("hop_h", 2),
    ("z3", 3), ("finish", 2), ("hop_h", 3), ("finish", 3),
)


def local(visibilities, col_offsets, row_offsets, facet_offsets, facet_order, vis_counts):
    vmem, smem = pltpu.VMEM, pltpu.SMEM
    scratch = [
        vmem((2, M, M), BF16),
        vmem((2, 4, 2, 2, CH, 2 * M), BF16),
        vmem((CH, M), F32), vmem((CH, M), F32),
        vmem((NCH, 4, 2, 2, CH, M), BF16),
        vmem((NCH, 4, 2, 2, CH, M), BF16),
        vmem((NCH, 4, 2, 2, CH, M), F32),
        *[vmem((NCH, 2, 2, CH, M), BF16) for _ in range(6)],
        vmem((NCH, 2, CH, M), BF16), vmem((NCH, 2, CH, M), BF16),
        vmem((NF, M), F32), vmem((NF, M), F32),
        vmem((NF, CH, 2 * M), BF16),
        vmem((2 * M, 2 * JB), BF16),
        vmem((NCH, 8, 2, CH, 2 * JB), F32),
        vmem((NCH, 2, 4, 2, CH, 2 * JB), BF16), vmem((NCH, 2, 4, 2, CH, 2 * JB), BF16),
        vmem((NCH, CH, 2 * JB), BF16), vmem((NCH, CH, 2 * JB), BF16),
        vmem((8, 128), F32), vmem((NF, 8, 128), F32),
        pltpu.SemaphoreType.DMA((2,)),
        pltpu.SemaphoreType.DMA((NCH, COPIES)), pltpu.SemaphoreType.DMA((NCH, COPIES)),
        pltpu.SemaphoreType.DMA((NF,)), pltpu.SemaphoreType.DMA((NF,)),
    ]
    return pl.pallas_call(
        body,
        out_shape=(jax.ShapeDtypeStruct((1, 2, FR, JB), F32), jax.ShapeDtypeStruct((1,), F32)),
        in_specs=[pl.BlockSpec(memory_space=pl.ANY)] + [pl.BlockSpec(memory_space=smem)] * 5,
        out_specs=(pl.BlockSpec(memory_space=vmem), pl.BlockSpec(memory_space=smem)),
        scratch_shapes=scratch,
        compiler_params=pltpu.CompilerParams(
            collective_id=0, has_side_effects=True, vmem_limit_bytes=56 * 1024 * 1024
        ),
        name="image_step",
    )(visibilities, col_offsets, row_offsets, facet_offsets, facet_order, vis_counts)


def solution(mesh):
    in_specs = (P(None, "col", "row"), P("col"), P(), P(), P(), P("col", "row"))
    out_specs = (P("col", None, None, "row"), P("col"))
    return jax.shard_map(local, mesh=mesh, in_specs=in_specs, out_specs=out_specs, check_vma=False)
```

time: 184 us -> 77.7 us (0.42); the launches traced: 181 us -> 77.5 us
  waiting for transfers between devices: 75.7 us -> 0 us
  Pallas kernels: 0 us -> 70.8 us
  blocking collectives: 37.8 us -> 0 us
  other arithmetic: 31.2 us -> 0 us
  matrix products: 17.1 us -> 0 us
  starting transfers between devices: 16.1 us -> 0 us
  local copies, waits for them, and re-layouts: 0.65 us -> 2.92 us
    all_to_all x2 -> x0, waiting for transfers between devices: 75.7 us -> none  [sent_and_summed(): arrived = lax.all_to_all(x, axis, split_axis=0, concat_axis=0, tiled=True)]
    pallas_call x0 -> x1, Pallas kernels: none -> 70.8 us  [local(): pl.pallas_call(body, out_shape=(jax.ShapeDtypeStruct((1, 2, FR, JB), F32)...]
    pmax x1 -> x0, blocking collectives: 37.8 us -> none  [local(): peak = lax.pmax(jnp.max(magnitude)[None], 'row')]
    dot_general x2 -> x0, matrix products: 17.1 us -> none  [the longest x1 13.8 us: local(): jnp.dot(table.reshape(facets * 2 * FR, 2 * M), visibilities.reshape(2 * M...]
    all_to_all x2 -> x0, starting transfers between devices: 16.1 us -> none  [sent_and_summed(): arrived = lax.all_to_all(x, axis, split_axis=0, concat_axis=0, tiled=True)]
    another operation x3 -> x0, other arithmetic: 9.84 us -> none  [the longest x2 8.52 us: local(): jnp.stack([jnp.concatenate([re, -im], axis=-1), jnp.concatenate([im, re],...]
    convert_element_type x4 -> x0, other arithmetic: 7.05 us -> none  [the longest x1 5 us: local(): fine[1].astype(jnp.bfloat16)]
    neg x2 -> x0, other arithmetic: 5.07 us -> none  [the longest x1 4.42 us: local(): -fine_im]
  transfers between devices with their start and end apart: 2 -> 0, of which waited for: 2 -> 0; matrix products, arithmetic and copies ran while one was open for 7% -> 0% of each run, Pallas kernels for 0% -> 0%
where the time goes in v2:
time: 77.7 us; the launch traced here: 77.5 us
  Pallas kernels  70.8 us (91%)
  between operations  3.74 us (5%)
  local copies, waits for them, and re-layouts  2.92 us (4%)
    pallas_call x1, Pallas kernels, local(): pl.pallas_call(body, out_shape=(jax.ShapeDtypeStruct((1, 2, FR, JB), F32)...  70.8 us
    unnamed x2, local copies, waits for them, and re-layouts  2.92 us

profile of v2, /device:TPU:8, one launch (start us, length us, event | category | flops | bytes accessed | tf_op | source)
XLA Modules:
  0.0 77.5 jit_solution(5978715453992697568)
XLA Ops:
  1.9 1.4 %copy.8.facet_offsets = s32[16,2]{1,0:T(8,128)} copy(s32[16,2]{0,1:T(2,128)} %param.9) | data formatting | bytes 256 | tf_op args[3]
  3.3 70.8 %image_step.1 = (f32[1,2,64,256]{3,2,1,0:T(8,128)}, f32[1]{0:T(128)}) custom-call(bf16[2,1024,1024]{2,1,0:T(8,128)(2,1)} %vis.1, s32[1]{0:T(128)S(6)} %copy.11.col_offsets, s32[16]{0:T(128)} %row_offsets.1, s32[16,2]{1,0:T(8,128)} %copy.8.facet_offsets, s32[16]{0:T(128)} %facet_order.1, s32[1,1]{1,0:T(1,128)S(6)} %copy.12.vis_counts), custom_call_target="tpu_custom_call" | custom-call | tf_op jit(solution)/shard_map/image_step/pallas_call | solution.py:312
  74.1 1.6 %copy.13 = f32[1,2,64,256]{3,2,1,0:T(8,128)} copy(f32[1,2,64,256]{3,2,1,0:T(8,128)} %get-tuple-element.4) | data formatting | bytes 262144

commit v3 on v2

v3 whole, which is shorter than its diff:
```python
import math

import jax
import jax.numpy as jnp
from jax import lax
from jax.experimental import pallas as pl
from jax.experimental.pallas import tpu as pltpu
from jax.sharding import PartitionSpec as P

MESH = pl.DeviceIdType.MESH
F32, BF16, I32 = jnp.float32, jnp.bfloat16, jnp.int32

M = 1024
FS = 4096
NG = 16384
FR = 64
NF = 16
CH = 16
NCH = FR // CH
JB = FS // NF
TWO_PI = 2.0 * math.pi
BEAM_SLOPE = 0.66
FIRST_SCALE = 1.0 / math.sqrt(NG)
SECOND_SCALE = 0.5 / math.sqrt(NG)

LA = 640
LB = M - LA

NAMES = (
    "core", "xa_up", "xa_dn", "xb_up", "xb_dn", "xc_up", "xc_dn", "y",
    "yb", "ua_up", "ua_dn", "ub_up", "ub_dn", "uc_up", "uc_dn",
    "z3_up", "z3_dn", "z4_up", "z4_dn", "z1_up", "z1_dn", "z2_up", "z2_dn", "h",
)


def wave(exponent):
    angle = (exponent & (NG - 1)).astype(F32) * (TWO_PI / NG)
    return jnp.cos(angle), jnp.sin(angle)


def times(a, b):
    return a[0] * b[0] - a[1] * b[1], a[0] * b[1] + a[1] * b[0]


def iota(shape, dim):
    return lax.broadcasted_iota(I32, shape, dim)


def column_of(scalars, shape):
    row = iota(shape, 0)
    picked = jnp.zeros(shape, I32)
    for index, value in enumerate(scalars):
        picked = jnp.where(row == index, value, picked)
    return picked


def body(
    vis, col_offsets, row_offsets, facet_offsets, facet_order, vis_counts,
    out, peak,
    grid, table, unit_re, unit_im, part, part_in, own,
    xa_send, xb_send, xc_send, xa_recv, xb_recv, xc_recv, y_send, y_recv,
    yb_send, yb_recv, ua_send, ub_send, uc_send, ua_recv, ub_recv, uc_recv,
    twist_re, twist_im, left, fine, image, z_send, z_recv, z4_send, z4_recv, h_send, h_recv,
    result, top, tops,
    load_sem, store_sem, send_sem, recv_sem, top_send, top_recv,
):
    c, r = lax.axis_index("col"), lax.axis_index("row")
    x, ylo, core = c // 4, (c // 2) % 2, c % 2
    z, yhi = r // 2, r % 2
    to_core = (c + 1 - 2 * core, r)
    to_ylo = (c + 2 - 4 * ylo, r)
    to_yhi = (c, r + 1 - 2 * yhi)
    x_up, x_dn = ((c + 4) % 16, r), ((c + 12) % 16, r)
    z_up, z_dn = (c, (r + 2) % 16), (c, (r + 14) % 16)
    z_up2, z_dn2 = (c, (r + 4) % 16), (c, (r + 12) % 16)
    near = (to_core, to_ylo, x_up, x_dn, z_up, z_dn, z_up2, z_dn2, to_yhi)

    loads = [pltpu.make_async_copy(vis.at[p], grid.at[p], load_sem.at[p]) for p in range(2)]
    for load in loads:
        load.start()
    barrier = pltpu.get_barrier_semaphore()
    for peer in near:
        pl.semaphore_signal(barrier, inc=1, device_id=peer, device_id_type=MESH)

    started = []
    copies = [dict() for _ in range(NCH)]

    def send(k, name, src, dst, peer):
        index = NAMES.index(name)
        copy = pltpu.make_async_remote_copy(
            src_ref=src, dst_ref=dst, send_sem=send_sem.at[k, index], recv_sem=recv_sem.at[k, index],
            device_id=peer, device_id_type=MESH,
        )
        copy.start()
        started.append(copy)
        copies[k][name] = copy

    def arrived(k, *names):
        for name in names:
            copies[k][name].wait_recv()

    slots = [
        ((x + dx) % 4) * 4 + ((ylo + dy) % 2) * 2 + (core + 1 - half) % 2
        for half in range(2) for dx in range(4) for dy in range(2)
    ]
    rows_at = [facet_offsets[0, facet_order[s]] + (FS // 2 - FR // 2) for s in slots]
    wide = (NF, M)
    place = iota(wide, 1)
    grid_u = col_offsets[0] + place
    live = (place < vis_counts[0, 0]).astype(F32) * FIRST_SCALE
    slot_rows = column_of(rows_at, wide)
    unit = wave(grid_u * iota(wide, 0))
    unit_re[...], unit_im[...] = unit

    def build(k):
        base = wave(grid_u * ((slot_rows + CH * k) & (NG - 1)))
        base = (base[0] * live, base[1] * live)
        for half in range(2):
            for dx in range(4):
                for dy in range(2):
                    s = half * 8 + dx * 2 + dy
                    re, im = times((base[0][s : s + 1], base[1][s : s + 1]), (unit_re[...], unit_im[...]))
                    re, im = re.astype(BF16), im.astype(BF16)
                    table[half, dx, 0, dy, :, :M] = re
                    table[half, dx, 0, dy, :, M:] = -im
                    table[half, dx, 1, dy, :, :M] = im
                    table[half, dx, 1, dy, :, M:] = re

    def multiply(half):
        return jnp.dot(
            table[half].reshape(16 * CH, 2 * M), grid[...].reshape(2 * M, M), preferred_element_type=F32
        ).reshape(4, 2, 2, CH, M)

    def first_p(k):
        build(k)
        if k == 0:
            for load in loads:
                load.wait()
        part[k] = multiply(0).astype(BF16)
        if k == 0:
            pl.semaphore_wait(barrier, len(near))
        send(k, "core", part.at[k], part_in.at[k], to_core)

    def first_o(k):
        own[k] = multiply(1)

    A, B = slice(0, LA), slice(LA, M)

    def spread(k):
        arrived(k, "core")

        def both(dx, part_of, dy, lanes):
            return own[k, dx, part_of, dy, :, lanes] + part_in[k, dx, part_of, dy, :, lanes].astype(F32)

        def both_rows(dx, part_of):
            return own[k, dx, part_of, :, :, A] + part_in[k, dx, part_of, :, :, A].astype(F32)

        xa_send[k, 0] = both_rows(2, 0).astype(BF16)
        send(k, "xa_up", xa_send.at[k, 0], xa_recv.at[k, 0], x_up)
        xa_send[k, 1] = both_rows(2, 1).astype(BF16)
        send(k, "xa_dn", xa_send.at[k, 1], xa_recv.at[k, 1], x_dn)
        for dx in range(4):
            for q in range(2):
                yb_send[k, dx, q] = both(dx, q, 1, B).astype(BF16)
        send(k, "yb", yb_send.at[k], yb_recv.at[k], to_ylo)
        xb_send[k, 0] = both_rows(1, 1).astype(BF16)
        send(k, "xb_up", xb_send.at[k, 0], xb_recv.at[k, 0], x_up)
        xb_send[k, 1] = both_rows(3, 0).astype(BF16)
        send(k, "xb_dn", xb_send.at[k, 1], xb_recv.at[k, 1], x_dn)
        own[k, 1, 0, :, :, A] = both_rows(1, 0)
        own[k, 3, 1, :, :, A] = both_rows(3, 1)
        own[k, 0, 0, :, :, A] = both_rows(0, 0)
        own[k, 0, 1, :, :, A] = both_rows(0, 1)
        for dx in range(4):
            for q in range(2):
                own[k, dx, q, 0, :, B] = both(dx, q, 0, B)

    def relay_a(k):
        arrived(k, "xa_up")
        xc_send[k, 0] = (own[k, 1, 0, :, :, A] + xa_recv[k, 0].astype(F32)).astype(BF16)
        send(k, "xc_up", xc_send.at[k, 0], xc_recv.at[k, 0], x_up)
        arrived(k, "xa_dn")
        xc_send[k, 1] = (own[k, 3, 1, :, :, A] + xa_recv[k, 1].astype(F32)).astype(BF16)
        send(k, "xc_dn", xc_send.at[k, 1], xc_recv.at[k, 1], x_dn)

    def relay_b(k):
        arrived(k, "yb")

        def both(dx, q):
            return own[k, dx, q, 0, :, B] + yb_recv[k, dx, q].astype(F32)

        ua_send[k, 0] = both(2, 0).astype(BF16)
        send(k, "ua_up", ua_send.at[k, 0], ua_recv.at[k, 0], x_up)
        ua_send[k, 1] = both(2, 1).astype(BF16)
        send(k, "ua_dn", ua_send.at[k, 1], ua_recv.at[k, 1], x_dn)
        ub_send[k, 0] = both(1, 1).astype(BF16)
        send(k, "ub_up", ub_send.at[k, 0], ub_recv.at[k, 0], x_up)
        ub_send[k, 1] = both(3, 0).astype(BF16)
        send(k, "ub_dn", ub_send.at[k, 1], ub_recv.at[k, 1], x_dn)
        for dx, q in ((1, 0), (3, 1), (0, 0), (0, 1)):
            own[k, dx, q, 0, :, B] = both(dx, q)

    def hop_a(k):
        arrived(k, "xb_up", "xb_dn", "xc_up", "xc_dn")
        for q in range(2):
            y_send[k, q] = (
                own[k, 0, q, 1, :, A] + xb_recv[k, 1 - q, 1].astype(F32) + xc_recv[k, q, 1].astype(F32)
            ).astype(BF16)
        send(k, "y", y_send.at[k], y_recv.at[k], to_ylo)
        for q in range(2):
            own[k, 0, q, 0, :, A] = (
                own[k, 0, q, 0, :, A] + xb_recv[k, 1 - q, 0].astype(F32) + xc_recv[k, q, 0].astype(F32)
            )

    def hop_b(k):
        arrived(k, "ua_up")
        uc_send[k, 0] = (own[k, 1, 0, 0, :, B] + ua_recv[k, 0].astype(F32)).astype(BF16)
        send(k, "uc_up", uc_send.at[k, 0], uc_recv.at[k, 0], x_up)
        arrived(k, "ua_dn")
        uc_send[k, 1] = (own[k, 3, 1, 0, :, B] + ua_recv[k, 1].astype(F32)).astype(BF16)
        send(k, "uc_dn", uc_send.at[k, 1], uc_recv.at[k, 1], x_dn)

    def prepare(k):
        grid_v = row_offsets[r] + place
        start = facet_offsets[1, facet_order[c]]
        block = 2 * ((z + iota(wide, 0) // 2) % 8) + (yhi + iota(wide, 0)) % 2
        twist = wave(grid_v * ((start + JB * block) & (NG - 1)))
        twist_re[...] = twist[0] * SECOND_SCALE
        twist_im[...] = twist[1] * SECOND_SCALE
        shape = (32, JB)
        coarse = wave((row_offsets[r] + 32 * iota(shape, 0)) * iota(shape, 1))
        small = wave(iota(shape, 0) * iota(shape, 1))
        for v in range(32):
            re, im = times((coarse[0][v : v + 1], coarse[1][v : v + 1]), small)
            re, im = re.astype(BF16), im.astype(BF16)
            fine[32 * v : 32 * v + 32, :JB] = re
            fine[32 * v : 32 * v + 32, JB:] = im
            fine[M + 32 * v : M + 32 * v + 32, :JB] = -im
            fine[M + 32 * v : M + 32 * v + 32, JB:] = re

    UP, DN = slice(0, JB), slice(JB, 2 * JB)

    def second(k):
        arrived(k, "ub_up", "ub_dn", "uc_up", "uc_dn")
        for q in range(2):
            own[k, 0, q, 0, :, B] = (
                own[k, 0, q, 0, :, B] + ub_recv[k, 1 - q].astype(F32) + uc_recv[k, q].astype(F32)
            )
        arrived(k, "y")
        for q in range(2):
            own[k, 0, q, 0, :, A] = own[k, 0, q, 0, :, A] + y_recv[k, q].astype(F32)
        columns = (own[k, 0, 0, 0], own[k, 0, 1, 0])
        for b in range(NF):
            re, im = times(columns, (twist_re[b : b + 1, :], twist_im[b : b + 1, :]))
            left[b, :, :M] = re.astype(BF16)
            left[b, :, M:] = im.astype(BF16)
        image[k] = jnp.dot(
            left[...].reshape(NF * CH, 2 * M), fine[...], preferred_element_type=F32
        ).reshape(8, 2, CH, 2 * JB)
        for way, lanes, name, peer in ((0, UP, "z4_up", z_up2), (1, DN, "z4_dn", z_dn2)):
            z4_send[k, way] = image[k, 4, :, :, lanes].astype(BF16)
            send(k, name, z4_send.at[k, way], z4_recv.at[k, way], peer)
        for way, at, name, peer in (
            (0, 3, "z3_up", z_up), (1, 5, "z3_dn", z_dn), (0, 1, "z1_up", z_up), (1, 7, "z1_dn", z_dn),
        ):
            slot = 0 if name.startswith("z3") else 1
            z_send[k, way, slot] = image[k, at].astype(BF16)
            send(k, name, z_send.at[k, way, slot], z_recv.at[k, way, slot], peer)

    def relay_z(k):
        for way, at, up_or_dn, lanes, rest, peer in ((0, 2, "up", UP, DN, z_up2), (1, 6, "dn", DN, UP, z_dn2)):
            arrived(k, f"z3_{up_or_dn}", f"z4_{up_or_dn}")
            z_send[k, way, 2, :, :, lanes] = (
                image[k, at, :, :, lanes] + z_recv[k, way, 0, :, :, lanes].astype(F32) + z4_recv[k, way].astype(F32)
            ).astype(BF16)
            z_send[k, way, 2, :, :, rest] = (
                image[k, at, :, :, rest] + z_recv[k, way, 0, :, :, rest].astype(F32)
            ).astype(BF16)
            send(k, f"z2_{up_or_dn}", z_send.at[k, way, 2], z_recv.at[k, way, 2], peer)

    def hop_h(k):
        arrived(k, "z1_up", "z1_dn", "z2_up", "z2_dn")
        total = image[k, 0]
        for way in range(2):
            for slot in (1, 2):
                total = total + z_recv[k, way, slot].astype(F32)
        h_send[k] = total[1].astype(BF16)
        send(k, "h", h_send.at[k], h_recv.at[k], to_yhi)
        image[k, 0, 0] = total[0]

    stores = []

    def finish(k):
        column = (r * JB + iota((CH, JB), 1)).astype(F32)
        beam = 1.0 - BEAM_SLOPE * (column + 0.5) / FS
        arrived(k, "h")
        total = image[k, 0, 0] + h_recv[k].astype(F32)
        re, im = total[:, :JB] / beam, total[:, JB:] / beam
        rows = slice(CH * k, CH * k + CH)
        result[0, rows, :] = re
        result[1, rows, :] = im
        store = pltpu.make_async_copy(
            result.at[:, pl.ds(CH * k, CH), :], out.at[0, :, pl.ds(CH * k, CH), :], store_sem.at[k]
        )
        store.start()
        stores.append(store)
        power = re * re + im * im
        power = jnp.maximum(power[:8], power[8:])
        power = jnp.maximum(power[:, :128], power[:, 128:])
        top[...] = power if k == ORDER_FIRST else jnp.maximum(top[...], power)

    steps = {
        "first_p": first_p, "first_o": first_o, "spread": spread, "relay_a": relay_a, "relay_b": relay_b,
        "hop_a": hop_a, "hop_b": hop_b, "prepare": prepare, "second": second, "relay_z": relay_z,
        "hop_h": hop_h, "finish": finish,
    }
    for name, k in ORDER:
        with jax.named_scope(f"{name}_{k}"):
            steps[name](k)

    with jax.named_scope("peak"):
        sends = []
        for step in (8, 7, 9, 6, 10, 5, 11, 4, 12, 3, 13, 2, 14, 1, 15):
            copy = pltpu.make_async_remote_copy(
                src_ref=top, dst_ref=tops.at[step], send_sem=top_send.at[step], recv_sem=top_recv.at[step],
                device_id=(c, (r + step) % NF), device_id_type=MESH,
            )
            copy.start()
            sends.append(copy)
        best = top[...]
        for step in range(1, NF):
            sends[step - 1].wait_recv()
        for step in range(1, NF):
            best = jnp.maximum(best, tops[step])
        peak[0] = jnp.max(jnp.sqrt(best))
    with jax.named_scope("drain"):
        for store in stores:
            store.wait()
        for copy in started + sends:
            copy.wait_send()


ORDER = (
    ("first_p", 0), ("first_o", 0), ("first_p", 1), ("spread", 0), ("first_o", 1),
    ("spread", 1), ("first_p", 2), ("relay_a", 0), ("first_o", 2), ("relay_b", 0),
    ("relay_a", 1), ("spread", 2), ("first_p", 3), ("hop_a", 0), ("relay_b", 1),
    ("hop_b", 0), ("prepare", 0), ("hop_a", 1), ("first_o", 3), ("spread", 3),
    ("relay_a", 2), ("relay_b", 2), ("hop_b", 1), ("second", 0), ("relay_a", 3),
    ("relay_b", 3), ("hop_a", 2), ("hop_b", 2), ("relay_z", 0), ("second", 1),
    ("hop_a", 3), ("hop_b", 3), ("second", 2), ("second", 3), ("hop_h", 0),
    ("relay_z", 1), ("relay_z", 2), ("finish", 0), ("relay_z", 3), ("hop_h", 1),
    ("hop_h", 2), ("hop_h", 3), ("finish", 1), ("finish", 2), ("finish", 3),
)
ORDER_FIRST = 0


def local(visibilities, col_offsets, row_offsets, facet_offsets, facet_order, vis_counts):
    vmem, smem = pltpu.VMEM, pltpu.SMEM
    scratch = [
        vmem((2, M, M), BF16),
        vmem((2, 4, 2, 2, CH, 2 * M), BF16),
        vmem((CH, M), F32), vmem((CH, M), F32),
        vmem((NCH, 4, 2, 2, CH, M), BF16),
        vmem((NCH, 4, 2, 2, CH, M), BF16),
        vmem((NCH, 4, 2, 2, CH, M), F32),
        *[vmem((NCH, 2, 2, CH, LA), BF16) for _ in range(6)],
        vmem((NCH, 2, CH, LA), BF16), vmem((NCH, 2, CH, LA), BF16),
        vmem((NCH, 4, 2, CH, LB), BF16), vmem((NCH, 4, 2, CH, LB), BF16),
        *[vmem((NCH, 2, CH, LB), BF16) for _ in range(6)],
        vmem((NF, M), F32), vmem((NF, M), F32),
        vmem((NF, CH, 2 * M), BF16),
        vmem((2 * M, 2 * JB), BF16),
        vmem((NCH, 8, 2, CH, 2 * JB), F32),
        vmem((NCH, 2, 3, 2, CH, 2 * JB), BF16), vmem((NCH, 2, 3, 2, CH, 2 * JB), BF16),
        vmem((NCH, 2, 2, CH, JB), BF16), vmem((NCH, 2, 2, CH, JB), BF16),
        vmem((NCH, CH, 2 * JB), BF16), vmem((NCH, CH, 2 * JB), BF16),
        vmem((2, FR, JB), F32),
        vmem((8, 128), F32), vmem((NF, 8, 128), F32),
        pltpu.SemaphoreType.DMA((2,)), pltpu.SemaphoreType.DMA((NCH,)),
        pltpu.SemaphoreType.DMA((NCH, len(NAMES))), pltpu.SemaphoreType.DMA((NCH, len(NAMES))),
        pltpu.SemaphoreType.DMA((NF,)), pltpu.SemaphoreType.DMA((NF,)),
    ]
    return pl.pallas_call(
        body,
        out_shape=(jax.ShapeDtypeStruct((1, 2, FR, JB), F32), jax.ShapeDtypeStruct((1,), F32)),
        in_specs=[pl.BlockSpec(memory_space=pl.ANY)] + [pl.BlockSpec(memory_space=smem)] * 5,
        out_specs=(pl.BlockSpec(memory_space=pl.ANY), pl.BlockSpec(memory_space=smem)),
        scratch_shapes=scratch,
        compiler_params=pltpu.CompilerParams(
            collective_id=0, has_side_effects=True, vmem_limit_bytes=56 * 1024 * 1024
        ),
        name="image_step",
    )(visibilities, col_offsets, row_offsets, facet_offsets.T, facet_order, vis_counts)


def solution(mesh):
    in_specs = (P(None, "col", "row"), P("col"), P(), P(), P(), P("col", "row"))
    out_specs = (P("col", None, None, "row"), P("col"))
    return jax.shard_map(local, mesh=mesh, in_specs=in_specs, out_specs=out_specs, check_vma=False)
```

time: 77.7 us -> 60.7 us (0.78)
  Pallas kernels: 70.8 us -> 55.2 us
  local copies, waits for them, and re-layouts: 2.92 us -> 1.57 us
    pallas_call x1, Pallas kernels: 70.8 us -> 55.2 us  [local(): pl.pallas_call(body, out_shape=(jax.ShapeDtypeStruct((1, 2, FR, JB), F32)...]
    unnamed x2 -> x1, local copies, waits for them, and re-layouts: 2.92 us -> 1.57 us
where the time goes in v3:
time: 60.7 us; the launch traced here: 60.5 us
  Pallas kernels  55.2 us (91%)
  between operations  3.74 us (6%)
  local copies, waits for them, and re-layouts  1.57 us (3%)
    pallas_call x1, Pallas kernels, local(): pl.pallas_call(body, out_shape=(jax.ShapeDtypeStruct((1, 2, FR, JB), F32)...  55.2 us
    unnamed x1, local copies, waits for them, and re-layouts  1.57 us

profile of v3, /device:TPU:8, one launch (start us, length us, event | category | flops | bytes accessed | tf_op | source)
XLA Modules:
  0.0 60.5 jit_solution(16218113248140410006)
XLA Ops:
  1.9 55.2 %image_step.1 = (f32[1,2,64,256]{3,2,1,0:T(8,128)}, f32[1]{0:T(128)}) custom-call(bf16[2,1024,1024]{2,1,0:T(8,128)(2,1)} %vis.1, s32[1]{0:T(128)S(6)} %copy.10.col_offsets, s32[16]{0:T(128)} %row_offsets.1, s32[2,16]{1,0:T(2,128)} %bitcast.1, s32[16]{0:T(128)} %facet_order.1, s32[1,1]{1,0:T(1,128)S(6)} %copy.11.vis_counts), custom_call_target="tpu_custom_call" | custom-call | tf_op jit(solution)/shard_map/image_step/pallas_call | solution.py:383
  57.1 1.6 %copy.12 = f32[1,2,64,256]{3,2,1,0:T(8,128)} copy(f32[1,2,64,256]{3,2,1,0:T(8,128)} %get-tuple-element.4) | data formatting | bytes 262144

commit v4 on v1

v4 whole, which is shorter than its diff:
```python
import math

import jax
import jax.numpy as jnp
from jax import lax
from jax.experimental import pallas as pl
from jax.experimental.pallas import tpu as pltpu
from jax.sharding import PartitionSpec as P

MESH = pl.DeviceIdType.MESH
F32, BF16, I32 = jnp.float32, jnp.bfloat16, jnp.int32

M = 1024
FS = 4096
NG = 16384
FR = 64
NF = 16
CH = 8
NCH = FR // CH
TR = 2 * CH
JB = FS // NF
TWO_PI = 2.0 * math.pi
BEAM_SLOPE = 0.66
FIRST_SCALE = 1.0 / math.sqrt(NG)
SECOND_SCALE = 0.5 / math.sqrt(NG)

LA = 768
LB = M - LA
UA, UB = LA // 2, LB // 2

KINDS = ("core", "xa", "xr", "y", "yb", "ua", "ur", "zs", "zd", "h")


def wave(exponent):
    angle = (exponent & (NG - 1)).astype(F32) * (TWO_PI / NG)
    return jnp.cos(angle), jnp.sin(angle)


def times(a, b):
    return a[0] * b[0] - a[1] * b[1], a[0] * b[1] + a[1] * b[0]


def iota(shape, dim):
    return lax.broadcasted_iota(I32, shape, dim)


def column_of(scalars, shape):
    row = iota(shape, 0)
    picked = jnp.zeros(shape, I32)
    for index, value in enumerate(scalars):
        picked = jnp.where(row == index, value, picked)
    return picked


def body(
    vis, col_offsets, row_offsets, facet_offsets, facet_order, vis_counts,
    out, peak,
    grid, table, unit_re, unit_im, part, part_in, own,
    xa_send, xa_recv, xr_send, xr_recv, y_send, y_recv,
    yb_send, yb_recv, ua_send, ua_recv, ur_send, ur_recv,
    twist_re, twist_im, left, fine, image, zs_send, zs_recv, zd_send, zd_recv, h_send, h_recv,
    top, tops,
    load_sem, send_sem, recv_sem, top_send, top_recv,
):
    c, r = lax.axis_index("col"), lax.axis_index("row")
    x, ylo, core = c // 4, (c // 2) % 2, c % 2
    z, yhi = r // 2, r % 2
    to_core = (c + 1 - 2 * core, r)
    to_ylo = (c + 2 - 4 * ylo, r)
    to_yhi = (c, r + 1 - 2 * yhi)
    x_up, x_dn = ((c + 4) % 16, r), ((c + 12) % 16, r)
    z_up, z_dn = (c, (r + 2) % 16), (c, (r + 14) % 16)
    z_up2, z_dn2 = (c, (r + 4) % 16), (c, (r + 12) % 16)
    near = (to_core, to_ylo, x_up, x_dn, z_up, z_dn, z_up2, z_dn2, to_yhi)

    for p in range(2):
        for q in range(LOADS):
            rows = pl.ds(q * (M // LOADS), M // LOADS)
            pltpu.make_async_copy(vis.at[p, rows], grid.at[p, rows], load_sem).start()
    barrier = pltpu.get_barrier_semaphore()
    for peer in near:
        pl.semaphore_signal(barrier, inc=1, device_id=peer, device_id_type=MESH)

    def send(k, kind, src, dst, peer):
        index = KINDS.index(kind)
        pltpu.make_async_remote_copy(
            src_ref=src, dst_ref=dst, send_sem=send_sem.at[index], recv_sem=recv_sem.at[k, index],
            device_id=peer, device_id_type=MESH,
        ).start()

    buffers = {
        "core": (part, part_in), "xa": (xa_send, xa_recv), "xr": (xr_send, xr_recv), "y": (y_send, y_recv),
        "yb": (yb_send, yb_recv), "ua": (ua_send, ua_recv), "ur": (ur_send, ur_recv), "zs": (zs_send, zs_recv),
        "zd": (zd_send, zd_recv), "h": (h_send, h_recv),
    }

    def arrived(k, kind):
        index, (src, dst) = KINDS.index(kind), buffers[kind]
        pltpu.make_async_remote_copy(
            src_ref=src.at[k], dst_ref=dst.at[k], send_sem=send_sem.at[index], recv_sem=recv_sem.at[k, index],
            device_id=to_core, device_id_type=MESH,
        ).wait_recv()

    slots = [
        ((x + dx) % 4) * 4 + ((ylo + dy) % 2) * 2 + (core + 1 - half) % 2
        for half in range(2) for dx in range(4) for dy in range(2)
    ]
    rows_at = [facet_offsets[0, facet_order[s]] + (FS // 2 - FR // 2) for s in slots]
    wide = (NF, M)
    place = iota(wide, 1)
    grid_u = col_offsets[0] + place
    live = (place < vis_counts[0, 0]).astype(F32) * FIRST_SCALE
    slot_rows = column_of(rows_at, wide)
    unit = wave(grid_u[:CH] * iota((CH, M), 0))
    unit_re[...], unit_im[...] = unit

    def first(k):
        base = wave(grid_u * ((slot_rows + CH * k) & (NG - 1)))
        base = (base[0] * live, base[1] * live)
        for s in range(NF):
            re, im = times((base[0][s : s + 1], base[1][s : s + 1]), (unit_re[...], unit_im[...]))
            table[s, :, :M] = jnp.concatenate([re, im], axis=0).astype(BF16)
            table[s, :, M:] = jnp.concatenate([-im, re], axis=0).astype(BF16)
        if k == 0:
            pltpu.make_async_copy(vis, grid, load_sem).wait()
        product = jnp.dot(
            table[...].reshape(NF * TR, 2 * M), grid[...].reshape(2 * M, M), preferred_element_type=F32
        ).reshape(2, 4, 2, TR, M)
        part[k] = product[0].astype(BF16)
        if k == 0:
            pl.semaphore_wait(barrier, len(near))
        send(k, "core", part.at[k], part_in.at[k], to_core)
        own[k] = product[1]

    A, B = slice(0, LA), slice(LA, M)
    A_UP, A_DN, B_UP, B_DN = slice(0, UA), slice(UA, LA), slice(LA, LA + UB), slice(LA + UB, M)
    UP_A, DN_A, UP_B, DN_B = pl.ds(0, UA), pl.ds(UA, LA - UA), pl.ds(0, UB), pl.ds(UB, LB - UB)

    def spread(k):
        arrived(k, "core")

        def both(dx, lanes, dy=slice(0, 2)):
            return own[k, dx, dy, :, lanes] + part_in[k, dx, dy, :, lanes].astype(F32)

        xa_send[k] = both(2, A).astype(BF16)
        send(k, "xa", xa_send.at[k, :, :, UP_A], xa_recv.at[k, :, :, UP_A], x_up)
        send(k, "xa", xa_send.at[k, :, :, DN_A], xa_recv.at[k, :, :, DN_A], x_dn)
        for dx in range(4):
            yb_send[k, dx] = both(dx, B, 1).astype(BF16)
        send(k, "yb", yb_send.at[k], yb_recv.at[k], to_ylo)
        xr_send[k, 0, :, :, A_DN] = both(1, A_DN).astype(BF16)
        send(k, "xr", xr_send.at[k, 0, :, :, DN_A], xr_recv.at[k, 0, :, :, DN_A], x_up)
        xr_send[k, 0, :, :, A_UP] = both(3, A_UP).astype(BF16)
        send(k, "xr", xr_send.at[k, 0, :, :, UP_A], xr_recv.at[k, 0, :, :, UP_A], x_dn)
        own[k, 1, :, :, A_UP] = both(1, A_UP)
        own[k, 3, :, :, A_DN] = both(3, A_DN)
        own[k, 0, :, :, A] = both(0, A)
        for dx in range(4):
            own[k, dx, 0, :, B] = both(dx, B, 0)

    def relay_a(k):
        arrived(k, "xa")
        xr_send[k, 1, :, :, A_UP] = (own[k, 1, :, :, A_UP] + xa_recv[k, :, :, A_UP].astype(F32)).astype(BF16)
        send(k, "xr", xr_send.at[k, 1, :, :, UP_A], xr_recv.at[k, 1, :, :, UP_A], x_up)
        xr_send[k, 1, :, :, A_DN] = (own[k, 3, :, :, A_DN] + xa_recv[k, :, :, A_DN].astype(F32)).astype(BF16)
        send(k, "xr", xr_send.at[k, 1, :, :, DN_A], xr_recv.at[k, 1, :, :, DN_A], x_dn)

    def hop_a(k):
        arrived(k, "xr")

        def summed(dy):
            return own[k, 0, dy, :, A] + xr_recv[k, 0, dy].astype(F32) + xr_recv[k, 1, dy].astype(F32)

        y_send[k] = summed(1).astype(BF16)
        send(k, "y", y_send.at[k], y_recv.at[k], to_ylo)
        own[k, 0, 0, :, A] = summed(0)

    def relay_b(k):
        arrived(k, "yb")

        def both(dx, lanes, rows):
            return own[k, dx, 0, :, lanes] + yb_recv[k, dx, :, rows].astype(F32)

        up, dn = slice(0, UB), slice(UB, LB)
        ua_send[k] = both(2, B, slice(0, LB)).astype(BF16)
        send(k, "ua", ua_send.at[k, :, UP_B], ua_recv.at[k, :, UP_B], x_up)
        send(k, "ua", ua_send.at[k, :, DN_B], ua_recv.at[k, :, DN_B], x_dn)
        ur_send[k, 0, :, dn] = both(1, B_DN, dn).astype(BF16)
        send(k, "ur", ur_send.at[k, 0, :, DN_B], ur_recv.at[k, 0, :, DN_B], x_up)
        ur_send[k, 0, :, up] = both(3, B_UP, up).astype(BF16)
        send(k, "ur", ur_send.at[k, 0, :, UP_B], ur_recv.at[k, 0, :, UP_B], x_dn)
        own[k, 1, 0, :, B_UP] = both(1, B_UP, up)
        own[k, 3, 0, :, B_DN] = both(3, B_DN, dn)
        own[k, 0, 0, :, B] = both(0, B, slice(0, LB))

    def hop_b(k):
        arrived(k, "ua")
        up, dn = slice(0, UB), slice(UB, LB)
        ur_send[k, 1, :, up] = (own[k, 1, 0, :, B_UP] + ua_recv[k, :, up].astype(F32)).astype(BF16)
        send(k, "ur", ur_send.at[k, 1, :, UP_B], ur_recv.at[k, 1, :, UP_B], x_up)
        ur_send[k, 1, :, dn] = (own[k, 3, 0, :, B_DN] + ua_recv[k, :, dn].astype(F32)).astype(BF16)
        send(k, "ur", ur_send.at[k, 1, :, DN_B], ur_recv.at[k, 1, :, DN_B], x_dn)

    def prepare(k):
        grid_v = row_offsets[r] + place
        start = facet_offsets[1, facet_order[c]]
        block = 2 * ((z + iota(wide, 0) // 2) % 8) + (yhi + iota(wide, 0)) % 2
        twist = wave(grid_v * ((start + JB * block) & (NG - 1)))
        twist_re[...] = twist[0] * SECOND_SCALE
        twist_im[...] = twist[1] * SECOND_SCALE
        shape = (32, JB)
        coarse = wave((row_offsets[r] + 32 * iota(shape, 0)) * iota(shape, 1))
        small = wave(iota(shape, 0) * iota(shape, 1))
        for v in range(32):
            re, im = times((coarse[0][v : v + 1], coarse[1][v : v + 1]), small)
            re, im = re.astype(BF16), im.astype(BF16)
            fine[32 * v : 32 * v + 32, :JB] = re
            fine[32 * v : 32 * v + 32, JB:] = im
            fine[M + 32 * v : M + 32 * v + 32, :JB] = -im
            fine[M + 32 * v : M + 32 * v + 32, JB:] = re

    def second(k):
        arrived(k, "ur")
        right = own[k, 0, 0, :, B] + ur_recv[k, 0].astype(F32) + ur_recv[k, 1].astype(F32)
        arrived(k, "y")
        columns = jnp.concatenate([own[k, 0, 0, :, A] + y_recv[k].astype(F32), right], axis=1)
        columns = (columns[:CH], columns[CH:])
        for d in range(8):
            pair = [
                times(columns, (twist_re[b : b + 1, :], twist_im[b : b + 1, :])) for b in (2 * d, 2 * d + 1)
            ]
            for q in range(2):
                left[d, :, M * q : M * q + M] = jnp.concatenate([pair[0][q], pair[1][q]], axis=0).astype(BF16)
        image[k] = jnp.dot(
            left[...].reshape(NF * CH, 2 * M), fine[...], preferred_element_type=F32
        ).reshape(8, TR, 2 * JB)
        for way, at, half, peer, peer2 in ((0, 3, 0, z_up, z_up2), (1, 5, 1, z_dn, z_dn2)):
            zs_send[k, way, 2] = image[k, 4, :, JB * half : JB * half + JB].astype(BF16)
            send(k, "zs", zs_send.at[k, way, 2], zs_recv.at[k, way, 2], peer2)
            for q in range(2):
                zs_send[k, way, q] = image[k, at, :, JB * q : JB * q + JB].astype(BF16)
            send(k, "zs", zs_send.at[k, way, pl.ds(0, 2)], zs_recv.at[k, way, pl.ds(0, 2)], peer)
        for way, at, peer in ((0, 1, z_up), (1, 7, z_dn)):
            zd_send[k, way] = image[k, at].astype(BF16)
            send(k, "zd", zd_send.at[k, way], zd_recv.at[k, way], peer)

    def relay_z(k):
        arrived(k, "zs")
        for way, at, half, peer in ((0, 2, 0, z_up2), (1, 6, 1, z_dn2)):
            for q in range(2):
                lanes = slice(JB * q, JB * q + JB)
                total = image[k, at, :, lanes] + zs_recv[k, way, q].astype(F32)
                if q == half:
                    total = total + zs_recv[k, way, 2].astype(F32)
                zd_send[k, 2 + way, :, lanes] = total.astype(BF16)
            send(k, "zd", zd_send.at[k, 2 + way], zd_recv.at[k, 2 + way], peer)

    def hop_h(k):
        arrived(k, "zd")
        total = image[k, 0]
        for way in range(4):
            total = total + zd_recv[k, way].astype(F32)
        h_send[k] = jnp.concatenate([total[CH:, :JB], total[CH:, JB:]], axis=0).astype(BF16)
        send(k, "h", h_send.at[k], h_recv.at[k], to_yhi)
        image[k, 0, :CH] = total[:CH]

    def finish(k):
        column = (r * JB + iota((CH, JB), 1)).astype(F32)
        beam = 1.0 - BEAM_SLOPE * (column + 0.5) / FS
        arrived(k, "h")
        total = h_recv[k].astype(F32)
        re = (image[k, 0, :CH, :JB] + total[:CH]) / beam
        im = (image[k, 0, :CH, JB:] + total[CH:]) / beam
        rows = slice(CH * k, CH * k + CH)
        out[0, 0, rows, :] = re
        out[0, 1, rows, :] = im
        power = re * re + im * im
        power = jnp.maximum(power[:, :128], power[:, 128:])
        top[...] = power if k == ORDER_FIRST else jnp.maximum(top[...], power)

    steps = {
        "first": first, "spread": spread, "relay_a": relay_a, "relay_b": relay_b, "hop_a": hop_a, "hop_b": hop_b,
        "prepare": prepare, "second": second, "relay_z": relay_z, "hop_h": hop_h, "finish": finish,
    }
    for name, k in ORDER:
        with jax.named_scope(f"{name}_{k}"):
            steps[name](k)

    with jax.named_scope("peak"):
        for step in (8, 7, 9, 6, 10, 5, 11, 4, 12, 3, 13, 2, 14, 1, 15):
            pltpu.make_async_remote_copy(
                src_ref=top, dst_ref=tops.at[step - 1], send_sem=top_send, recv_sem=top_recv,
                device_id=(c, (r + step) % NF), device_id_type=MESH,
            ).start()
        all_tops = pltpu.make_async_remote_copy(
            src_ref=tops, dst_ref=tops, send_sem=top_send, recv_sem=top_recv, device_id=to_core, device_id_type=MESH
        )
        all_tops.wait_recv()
        best = top[...]
        for step in range(NF - 1):
            best = jnp.maximum(best, tops[step])
        peak[...] = jnp.full((8, 128), jnp.max(jnp.sqrt(best)))
    with jax.named_scope("drain"):
        all_tops.wait_send()
        for index, kind in enumerate(KINDS):
            src, dst = buffers[kind]
            pltpu.make_async_remote_copy(
                src_ref=src, dst_ref=dst, send_sem=send_sem.at[index], recv_sem=recv_sem.at[0, index],
                device_id=to_core, device_id_type=MESH,
            ).wait_send()


LOADS = 4
ORDER = (
    ("first", 0), ("first", 1), ("spread", 0), ("first", 2), ("spread", 1),
    ("first", 3), ("spread", 2), ("relay_a", 0), ("first", 4), ("relay_b", 0),
    ("relay_a", 1), ("relay_b", 1), ("spread", 3), ("first", 5), ("relay_a", 2),
    ("relay_b", 2), ("spread", 4), ("first", 6), ("hop_a", 0), ("hop_b", 0),
    ("hop_b", 1), ("hop_a", 1), ("spread", 5), ("relay_b", 3), ("first", 7),
    ("relay_a", 3), ("hop_b", 2), ("relay_b", 4), ("spread", 6), ("hop_a", 2),
    ("prepare", 0), ("relay_a", 4), ("second", 0), ("relay_a", 5), ("second", 1),
    ("spread", 7), ("hop_b", 3), ("hop_a", 3), ("relay_b", 5), ("second", 2),
    ("relay_a", 6), ("relay_b", 6), ("relay_z", 0), ("hop_b", 4), ("hop_a", 4),
    ("hop_a", 5), ("relay_a", 7), ("relay_z", 1), ("hop_b", 5), ("relay_b", 7),
    ("second", 3), ("hop_a", 6), ("hop_b", 6), ("relay_z", 2), ("second", 4),
    ("hop_a", 7), ("hop_b", 7), ("second", 5), ("second", 6), ("relay_z", 3),
    ("second", 7), ("relay_z", 5), ("relay_z", 4), ("relay_z", 6), ("relay_z", 7),
    ("hop_h", 3), ("hop_h", 5), ("hop_h", 1), ("hop_h", 4), ("hop_h", 2),
    ("hop_h", 6), ("hop_h", 0), ("hop_h", 7), ("finish", 5), ("finish", 1),
    ("finish", 3), ("finish", 6), ("finish", 0), ("finish", 2), ("finish", 4),
    ("finish", 7),
)
ORDER_FIRST = 5


def local(visibilities, col_offsets, row_offsets, facet_offsets, facet_order, vis_counts):
    vmem, smem = pltpu.VMEM, pltpu.SMEM

    def twice(*shape):
        return [vmem((NCH, *shape), BF16), vmem((NCH, *shape), BF16)]

    scratch = [
        vmem((2, M, M), BF16),
        vmem((NF, TR, 2 * M), BF16),
        vmem((CH, M), F32), vmem((CH, M), F32),
        *twice(4, 2, TR, M),
        vmem((NCH, 4, 2, TR, M), F32),
        *twice(2, TR, LA), *twice(2, 2, TR, LA), *twice(TR, LA),
        *twice(4, TR, LB), *twice(TR, LB), *twice(2, TR, LB),
        vmem((NF, M), F32), vmem((NF, M), F32),
        vmem((8, TR, 2 * M), BF16),
        vmem((2 * M, 2 * JB), BF16),
        vmem((NCH, 8, TR, 2 * JB), F32),
        *twice(2, 3, TR, JB), *twice(4, TR, 2 * JB), *twice(TR, JB),
        vmem((8, 128), F32), vmem((NF - 1, 8, 128), F32),
        pltpu.SemaphoreType.DMA,
        pltpu.SemaphoreType.DMA((len(KINDS),)), pltpu.SemaphoreType.DMA((NCH, len(KINDS))),
        pltpu.SemaphoreType.DMA, pltpu.SemaphoreType.DMA,
    ]
    images, peak = pl.pallas_call(
        body,
        out_shape=(vmem((1, 2, FR, JB), F32), vmem((8, 128), F32)),
        in_specs=[pl.BlockSpec(memory_space=pl.ANY)] + [pl.BlockSpec(memory_space=smem)] * 5,
        out_specs=(pl.BlockSpec(memory_space=vmem), pl.BlockSpec(memory_space=vmem)),
        scratch_shapes=scratch,
        compiler_params=pltpu.CompilerParams(
            collective_id=0, has_side_effects=True, vmem_limit_bytes=56 * 1024 * 1024
        ),
        name="image_step",
    )(visibilities, col_offsets, row_offsets, facet_offsets.T, facet_order, vis_counts)
    return images, peak[0, :1]


def solution(mesh):
    in_specs = (P(None, "col", "row"), P("col"), P(), P(), P(), P("col", "row"))
    out_specs = (P("col", None, None, "row"), P("col"))
    return jax.shard_map(local, mesh=mesh, in_specs=in_specs, out_specs=out_specs, check_vma=False)
```

time: 184 us -> 56.6 us (0.31); the launches traced: 181 us -> 56.4 us
  waiting for transfers between devices: 75.7 us -> 0 us
  Pallas kernels: 0 us -> 53.3 us
  blocking collectives: 37.8 us -> 0 us
  other arithmetic: 31.2 us -> 0 us
  matrix products: 17.1 us -> 0 us
  starting transfers between devices: 16.1 us -> 0 us
    all_to_all x2 -> x0, waiting for transfers between devices: 75.7 us -> none  [sent_and_summed(): arrived = lax.all_to_all(x, axis, split_axis=0, concat_axis=0, tiled=True)]
    pallas_call x0 -> x1, Pallas kernels: none -> 53.3 us  [local(): pl.pallas_call(body, out_shape=(vmem((1, 2, FR, JB), F32), vmem((8, 128),...]
    pmax x1 -> x0, blocking collectives: 37.8 us -> none  [local(): peak = lax.pmax(jnp.max(magnitude)[None], 'row')]
    dot_general x2 -> x0, matrix products: 17.1 us -> none  [the longest x1 13.8 us: local(): jnp.dot(table.reshape(facets * 2 * FR, 2 * M), visibilities.reshape(2 * M...]
    all_to_all x2 -> x0, starting transfers between devices: 16.1 us -> none  [sent_and_summed(): arrived = lax.all_to_all(x, axis, split_axis=0, concat_axis=0, tiled=True)]
    another operation x3 -> x0, other arithmetic: 9.84 us -> none  [the longest x2 8.52 us: local(): jnp.stack([jnp.concatenate([re, -im], axis=-1), jnp.concatenate([im, re],...]
    convert_element_type x4 -> x0, other arithmetic: 7.05 us -> none  [the longest x1 5 us: local(): fine[1].astype(jnp.bfloat16)]
    neg x2 -> x0, other arithmetic: 5.07 us -> none  [the longest x1 4.42 us: local(): -fine_im]
  transfers between devices with their start and end apart: 2 -> 0, of which waited for: 2 -> 0; matrix products, arithmetic and copies ran while one was open for 7% -> 0% of each run, Pallas kernels for 0% -> 0%
where the time goes in v4:
time: 56.6 us; the launch traced here: 56.4 us
  Pallas kernels  53.3 us (94%)
  between operations  1.93 us (3%)
  local copies, waits for them, and re-layouts  1.17 us (2%)
    pallas_call x1, Pallas kernels, local(): pl.pallas_call(body, out_shape=(vmem((1, 2, FR, JB), F32), vmem((8, 128),...  53.3 us

profile of v4, /device:TPU:8, one launch (start us, length us, event | category | flops | bytes accessed | tf_op | source)
XLA Modules:
  0.0 56.4 jit_solution(8251984151875154827)
XLA Ops:
  1.9 53.3 %image_step.1 = (f32[1,2,64,256]{3,2,1,0:T(8,128)S(1)}, f32[8,128]{1,0:T(8,128)S(1)}) custom-call(bf16[2,1024,1024]{2,1,0:T(8,128)(2,1)} %vis.1, s32[1]{0:T(128)S(6)} %copy.10.col_offsets, s32[16]{0:T(128)} %row_offsets.1, s32[2,16]{1,0:T(2,128)} %bitcast.2, s32[16]{0:T(128)} %facet_order.1, s32[1,1]{1,0:T(1,128)S(6)} %copy.11.vis_counts), custom_call_target="tpu_custom_call" | custom-call | tf_op jit(solution)/shard_map/image_step/pallas_call | solution.py:360
  55.2 0.5 slice.3
  55.7 0.7 %copy.9 = f32[1,2,64,256]{3,2,1,0:T(8,128)} copy(f32[1,2,64,256]{3,2,1,0:T(8,128)S(1)} %get-tuple-element.6) | data formatting | bytes 262144

commit v5 on v4

--- a/solution.py
+++ b/solution.py
@@ -24,9 +24,10 @@
 FIRST_SCALE = 1.0 / math.sqrt(NG)
 SECOND_SCALE = 0.5 / math.sqrt(NG)
 
-LA = 768
+LA = 640
 LB = M - LA
-UA, UB = LA // 2, LB // 2
+UP_LANES = ((384, 128), (256, 256))
+MERGED = (6, 7)
 
 KINDS = ("core", "xa", "xr", "y", "yb", "ua", "ur", "zs", "zd", "h")
 
@@ -55,10 +56,10 @@
 def body(
     vis, col_offsets, row_offsets, facet_offsets, facet_order, vis_counts,
     out, peak,
-    grid, table, unit_re, unit_im, part, part_in, own,
+    grid, table, unit_re, unit_im, base_re, base_im, turn_re, turn_im, part, part_in, own,
     xa_send, xa_recv, xr_send, xr_recv, y_send, y_recv,
     yb_send, yb_recv, ua_send, ua_recv, ur_send, ur_recv,
-    twist_re, twist_im, left, fine, image, zs_send, zs_recv, zd_send, zd_recv, h_send, h_recv,
+    twist_re, twist_im, left, fine, image, zs_send, zs_recv, zd_send, zd_recv, zm_send, zm_recv, h_send, h_recv,
     top, tops,
     load_sem, send_sem, recv_sem, top_send, top_recv,
 ):
@@ -71,7 +72,8 @@
     x_up, x_dn = ((c + 4) % 16, r), ((c + 12) % 16, r)
     z_up, z_dn = (c, (r + 2) % 16), (c, (r + 14) % 16)
     z_up2, z_dn2 = (c, (r + 4) % 16), (c, (r + 12) % 16)
-    near = (to_core, to_ylo, x_up, x_dn, z_up, z_dn, z_up2, z_dn2, to_yhi)
+    across = [(c, (2 * (z + d) + 1 - yhi) % 16) for d in (1, 7, 2, 6)]
+    near = (to_core, to_ylo, x_up, x_dn, z_up, z_dn, z_up2, z_dn2, to_yhi, *across)
 
     for p in range(2):
         for q in range(LOADS):
@@ -81,23 +83,32 @@
     for peer in near:
         pl.semaphore_signal(barrier, inc=1, device_id=peer, device_id_type=MESH)
 
+    def at(k, kind):
+        if kind == "zm":
+            return MERGED.index(k)
+        return NOT_MERGED.index(k) if kind in ("zd", "h") else k
+
+    def send_index(kind):
+        return len(KINDS) if kind == "zm" else KINDS.index(kind)
+
     def send(k, kind, src, dst, peer):
-        index = KINDS.index(kind)
         pltpu.make_async_remote_copy(
-            src_ref=src, dst_ref=dst, send_sem=send_sem.at[index], recv_sem=recv_sem.at[k, index],
+            src_ref=src, dst_ref=dst, send_sem=send_sem.at[send_index(kind)],
+            recv_sem=recv_sem.at[k, KINDS.index("zd" if kind == "zm" else kind)],
             device_id=peer, device_id_type=MESH,
         ).start()
 
     buffers = {
         "core": (part, part_in), "xa": (xa_send, xa_recv), "xr": (xr_send, xr_recv), "y": (y_send, y_recv),
         "yb": (yb_send, yb_recv), "ua": (ua_send, ua_recv), "ur": (ur_send, ur_recv), "zs": (zs_send, zs_recv),
-        "zd": (zd_send, zd_recv), "h": (h_send, h_recv),
+        "zd": (zd_send, zd_recv), "h": (h_send, h_recv), "zm": (zm_send, zm_recv),
     }
 
     def arrived(k, kind):
-        index, (src, dst) = KINDS.index(kind), buffers[kind]
+        src, dst = buffers[kind]
         pltpu.make_async_remote_copy(
-            src_ref=src.at[k], dst_ref=dst.at[k], send_sem=send_sem.at[index], recv_sem=recv_sem.at[k, index],
+            src_ref=src.at[at(k, kind)], dst_ref=dst.at[at(k, kind)], send_sem=send_sem.at[send_index(kind)],
+            recv_sem=recv_sem.at[k, KINDS.index("zd" if kind == "zm" else kind)],
             device_id=to_core, device_id_type=MESH,
         ).wait_recv()
 
@@ -111,32 +122,54 @@
     grid_u = col_offsets[0] + place
     live = (place < vis_counts[0, 0]).astype(F32) * FIRST_SCALE
     slot_rows = column_of(rows_at, wide)
-    unit = wave(grid_u[:CH] * iota((CH, M), 0))
-    unit_re[...], unit_im[...] = unit
-
-    def first(k):
-        base = wave(grid_u * ((slot_rows + CH * k) & (NG - 1)))
-        base = (base[0] * live, base[1] * live)
+    small = (CH, M)
+    for (re, im), wave_of in (
+        ((unit_re, unit_im), grid_u[:CH] * iota(small, 0)),
+        ((turn_re, turn_im), grid_u[:CH] * (CH * iota(small, 0))),
+        ((base_re, base_im), grid_u * (slot_rows & (NG - 1))),
+    ):
+        re[...], im[...] = wave(wave_of)
+    base_re[...], base_im[...] = base_re[...] * live, base_im[...] * live
+
+    def build(k):
+        turn = (turn_re[k : k + 1, :], turn_im[k : k + 1, :])
+        base = times((base_re[...], base_im[...]), turn) if k else (base_re[...], base_im[...])
         for s in range(NF):
             re, im = times((base[0][s : s + 1], base[1][s : s + 1]), (unit_re[...], unit_im[...]))
-            table[s, :, :M] = jnp.concatenate([re, im], axis=0).astype(BF16)
-            table[s, :, M:] = jnp.concatenate([-im, re], axis=0).astype(BF16)
+            table[k % 2, s, :, :M] = jnp.concatenate([re, im], axis=0).astype(BF16)
+            table[k % 2, s, :, M:] = jnp.concatenate([-im, re], axis=0).astype(BF16)
+
+    def multiply(rows):
+        return jnp.dot(rows.reshape(-1, 2 * M), grid[...].reshape(2 * M, M), preferred_element_type=F32)
+
+    def first(k):
         if k == 0:
+            build(0)
             pltpu.make_async_copy(vis, grid, load_sem).wait()
-        product = jnp.dot(
-            table[...].reshape(NF * TR, 2 * M), grid[...].reshape(2 * M, M), preferred_element_type=F32
-        ).reshape(2, 4, 2, TR, M)
+            part[0] = multiply(table[0, :8]).astype(BF16).reshape(4, 2, TR, M)
+            pl.semaphore_wait(barrier, len(near))
+            send(k, "core", part.at[k], part_in.at[k], to_core)
+            own[0] = multiply(table[0, 8:]).reshape(4, 2, TR, M)
+            build(1)
+            return
+        product = multiply(table[k % 2]).reshape(2, 4, 2, TR, M)
+        if k + 1 < NCH:
+            build(k + 1)
         part[k] = product[0].astype(BF16)
-        if k == 0:
-            pl.semaphore_wait(barrier, len(near))
+        own[k] = product[1]
         send(k, "core", part.at[k], part_in.at[k], to_core)
-        own[k] = product[1]
 
     A, B = slice(0, LA), slice(LA, M)
-    A_UP, A_DN, B_UP, B_DN = slice(0, UA), slice(UA, LA), slice(LA, LA + UB), slice(LA + UB, M)
-    UP_A, DN_A, UP_B, DN_B = pl.ds(0, UA), pl.ds(UA, LA - UA), pl.ds(0, UB), pl.ds(UB, LB - UB)
+
+    def halves(k):
+        ua, ub = UP_LANES[k % 2]
+        return (
+            (slice(0, ua), slice(ua, LA), slice(LA, LA + ub), slice(LA + ub, M)),
+            (pl.ds(0, ua), pl.ds(ua, LA - ua), pl.ds(0, ub), pl.ds(ub, LB - ub)),
+        )
 
     def spread(k):
+        (A_UP, A_DN, _, _), (UP_A, DN_A, _, _) = halves(k)
         arrived(k, "core")
 
         def both(dx, lanes, dy=slice(0, 2)):
@@ -159,6 +192,7 @@
             own[k, dx, 0, :, B] = both(dx, B, 0)
 
     def relay_a(k):
+        (A_UP, A_DN, _, _), (UP_A, DN_A, _, _) = halves(k)
         arrived(k, "xa")
         xr_send[k, 1, :, :, A_UP] = (own[k, 1, :, :, A_UP] + xa_recv[k, :, :, A_UP].astype(F32)).astype(BF16)
         send(k, "xr", xr_send.at[k, 1, :, :, UP_A], xr_recv.at[k, 1, :, :, UP_A], x_up)
@@ -176,12 +210,13 @@
         own[k, 0, 0, :, A] = summed(0)
 
     def relay_b(k):
+        (_, _, B_UP, B_DN), (_, _, UP_B, DN_B) = halves(k)
         arrived(k, "yb")
 
         def both(dx, lanes, rows):
             return own[k, dx, 0, :, lanes] + yb_recv[k, dx, :, rows].astype(F32)
 
-        up, dn = slice(0, UB), slice(UB, LB)
+        up, dn = slice(0, UP_LANES[k % 2][1]), slice(UP_LANES[k % 2][1], LB)
         ua_send[k] = both(2, B, slice(0, LB)).astype(BF16)
         send(k, "ua", ua_send.at[k, :, UP_B], ua_recv.at[k, :, UP_B], x_up)
         send(k, "ua", ua_send.at[k, :, DN_B], ua_recv.at[k, :, DN_B], x_dn)
@@ -194,8 +229,9 @@
         own[k, 0, 0, :, B] = both(0, B, slice(0, LB))
 
     def hop_b(k):
+        (_, _, B_UP, B_DN), (_, _, UP_B, DN_B) = halves(k)
         arrived(k, "ua")
-        up, dn = slice(0, UB), slice(UB, LB)
+        up, dn = slice(0, UP_LANES[k % 2][1]), slice(UP_LANES[k % 2][1], LB)
         ur_send[k, 1, :, up] = (own[k, 1, 0, :, B_UP] + ua_recv[k, :, up].astype(F32)).astype(BF16)
         send(k, "ur", ur_send.at[k, 1, :, UP_B], ur_recv.at[k, 1, :, UP_B], x_up)
         ur_send[k, 1, :, dn] = (own[k, 3, 0, :, B_DN] + ua_recv[k, :, dn].astype(F32)).astype(BF16)
@@ -234,43 +270,68 @@
         image[k] = jnp.dot(
             left[...].reshape(NF * CH, 2 * M), fine[...], preferred_element_type=F32
         ).reshape(8, TR, 2 * JB)
-        for way, at, half, peer, peer2 in ((0, 3, 0, z_up, z_up2), (1, 5, 1, z_dn, z_dn2)):
+        for way, dz, half, peer, peer2 in ((0, 3, 0, z_up, z_up2), (1, 5, 1, z_dn, z_dn2)):
             zs_send[k, way, 2] = image[k, 4, :, JB * half : JB * half + JB].astype(BF16)
             send(k, "zs", zs_send.at[k, way, 2], zs_recv.at[k, way, 2], peer2)
             for q in range(2):
-                zs_send[k, way, q] = image[k, at, :, JB * q : JB * q + JB].astype(BF16)
+                zs_send[k, way, q] = image[k, dz, :, JB * q : JB * q + JB].astype(BF16)
             send(k, "zs", zs_send.at[k, way, pl.ds(0, 2)], zs_recv.at[k, way, pl.ds(0, 2)], peer)
-        for way, at, peer in ((0, 1, z_up), (1, 7, z_dn)):
-            zd_send[k, way] = image[k, at].astype(BF16)
-            send(k, "zd", zd_send.at[k, way], zd_recv.at[k, way], peer)
+        for way, dz, peer in ((0, 1, z_up), (1, 7, z_dn)):
+            if k in MERGED:
+                merged_sends(k, way, image[k, dz], peer)
+            else:
+                n = at(k, "zd")
+                zd_send[n, way] = image[k, dz].astype(BF16)
+                send(k, "zd", zd_send.at[n, way], zd_recv.at[n, way], peer)
+        if k in MERGED:
+            n = at(k, "zm")
+            zm_send[n, 8] = folded(image[k, 0, CH:]).astype(BF16)
+            send(k, "zm", zm_send.at[n, 8], zm_recv.at[n, 8], to_yhi)
+
+    def folded(rows):
+        return jnp.concatenate([rows[:, :JB], rows[:, JB:]], axis=0)
+
+    def merged_sends(k, way, total, peer):
+        n = at(k, "zm")
+        for other, owner in ((1, across[way]), (0, peer)):
+            zm_send[n, 4 * other + way] = folded(total[CH * other : CH * other + CH]).astype(BF16)
+            send(k, "zm", zm_send.at[n, 4 * other + way], zm_recv.at[n, 4 * other + way], owner)
 
     def relay_z(k):
         arrived(k, "zs")
-        for way, at, half, peer in ((0, 2, 0, z_up2), (1, 6, 1, z_dn2)):
-            for q in range(2):
-                lanes = slice(JB * q, JB * q + JB)
-                total = image[k, at, :, lanes] + zs_recv[k, way, q].astype(F32)
-                if q == half:
-                    total = total + zs_recv[k, way, 2].astype(F32)
-                zd_send[k, 2 + way, :, lanes] = total.astype(BF16)
-            send(k, "zd", zd_send.at[k, 2 + way], zd_recv.at[k, 2 + way], peer)
+        for way, dz, half, peer in ((0, 2, 0, z_up2), (1, 6, 1, z_dn2)):
+            total = [image[k, dz, :, JB * q : JB * q + JB] + zs_recv[k, way, q].astype(F32) for q in range(2)]
+            total[half] = total[half] + zs_recv[k, way, 2].astype(F32)
+            if k in MERGED:
+                merged_sends(k, 2 + way, jnp.concatenate(total, axis=1), peer)
+            else:
+                n = at(k, "zd")
+                for q in range(2):
+                    zd_send[n, 2 + way, :, JB * q : JB * q + JB] = total[q].astype(BF16)
+                send(k, "zd", zd_send.at[n, 2 + way], zd_recv.at[n, 2 + way], peer)
 
     def hop_h(k):
         arrived(k, "zd")
-        total = image[k, 0]
+        total, n = image[k, 0], at(k, "zd")
         for way in range(4):
-            total = total + zd_recv[k, way].astype(F32)
-        h_send[k] = jnp.concatenate([total[CH:, :JB], total[CH:, JB:]], axis=0).astype(BF16)
-        send(k, "h", h_send.at[k], h_recv.at[k], to_yhi)
+            total = total + zd_recv[n, way].astype(F32)
+        h_send[n] = folded(total[CH:]).astype(BF16)
+        send(k, "h", h_send.at[n], h_recv.at[n], to_yhi)
         image[k, 0, :CH] = total[:CH]
 
     def finish(k):
-        column = (r * JB + iota((CH, JB), 1)).astype(F32)
+        column = (r * JB + iota((TR, JB), 1)).astype(F32)
         beam = 1.0 - BEAM_SLOPE * (column + 0.5) / FS
-        arrived(k, "h")
-        total = h_recv[k].astype(F32)
-        re = (image[k, 0, :CH, :JB] + total[:CH]) / beam
-        im = (image[k, 0, :CH, JB:] + total[CH:]) / beam
+        total = folded(image[k, 0, :CH])
+        if k in MERGED:
+            arrived(k, "zm")
+            for n in range(9):
+                total = total + zm_recv[at(k, "zm"), n].astype(F32)
+        else:
+            arrived(k, "h")
+            total = total + h_recv[at(k, "h")].astype(F32)
+        total = total / beam
+        re, im = total[:CH], total[CH:]
         rows = slice(CH * k, CH * k + CH)
         out[0, 0, rows, :] = re
         out[0, 1, rows, :] = im
@@ -302,46 +363,48 @@
         peak[...] = jnp.full((8, 128), jnp.max(jnp.sqrt(best)))
     with jax.named_scope("drain"):
         all_tops.wait_send()
-        for index, kind in enumerate(KINDS):
-            src, dst = buffers[kind]
+        for kind, (src, dst) in buffers.items():
+            index = 0
             pltpu.make_async_remote_copy(
-                src_ref=src, dst_ref=dst, send_sem=send_sem.at[index], recv_sem=recv_sem.at[0, index],
+                src_ref=src, dst_ref=dst, send_sem=send_sem.at[send_index(kind)], recv_sem=recv_sem.at[0, index],
                 device_id=to_core, device_id_type=MESH,
             ).wait_send()
 
 
 LOADS = 4
+NOT_MERGED = tuple(k for k in range(NCH) if k not in MERGED)
 ORDER = (
-    ("first", 0), ("first", 1), ("spread", 0), ("first", 2), ("spread", 1),
-    ("first", 3), ("spread", 2), ("relay_a", 0), ("first", 4), ("relay_b", 0),
-    ("relay_a", 1), ("relay_b", 1), ("spread", 3), ("first", 5), ("relay_a", 2),
-    ("relay_b", 2), ("spread", 4), ("first", 6), ("hop_a", 0), ("hop_b", 0),
-    ("hop_b", 1), ("hop_a", 1), ("spread", 5), ("relay_b", 3), ("first", 7),
-    ("relay_a", 3), ("hop_b", 2), ("relay_b", 4), ("spread", 6), ("hop_a", 2),
-    ("prepare", 0), ("relay_a", 4), ("second", 0), ("relay_a", 5), ("second", 1),
-    ("spread", 7), ("hop_b", 3), ("hop_a", 3), ("relay_b", 5), ("second", 2),
-    ("relay_a", 6), ("relay_b", 6), ("relay_z", 0), ("hop_b", 4), ("hop_a", 4),
-    ("hop_a", 5), ("relay_a", 7), ("relay_z", 1), ("hop_b", 5), ("relay_b", 7),
-    ("second", 3), ("hop_a", 6), ("hop_b", 6), ("relay_z", 2), ("second", 4),
-    ("hop_a", 7), ("hop_b", 7), ("second", 5), ("second", 6), ("relay_z", 3),
-    ("second", 7), ("relay_z", 5), ("relay_z", 4), ("relay_z", 6), ("relay_z", 7),
-    ("hop_h", 3), ("hop_h", 5), ("hop_h", 1), ("hop_h", 4), ("hop_h", 2),
-    ("hop_h", 6), ("hop_h", 0), ("hop_h", 7), ("finish", 5), ("finish", 1),
-    ("finish", 3), ("finish", 6), ("finish", 0), ("finish", 2), ("finish", 4),
-    ("finish", 7),
+    ("prepare", 0), ("first", 0), ("first", 1), ("spread", 0), ("first", 2),
+    ("spread", 1), ("first", 3), ("spread", 2), ("relay_a", 0), ("first", 4),
+    ("relay_b", 0), ("relay_a", 1), ("relay_b", 1), ("spread", 3), ("first", 5),
+    ("relay_a", 2), ("relay_b", 2), ("hop_a", 0), ("hop_b", 0), ("spread", 4),
+    ("first", 6), ("hop_b", 1), ("hop_a", 1), ("spread", 5), ("relay_a", 3),
+    ("first", 7), ("hop_b", 2), ("hop_a", 2), ("relay_b", 3), ("spread", 6),
+    ("relay_a", 4), ("second", 0), ("relay_b", 4), ("relay_a", 5), ("spread", 7),
+    ("second", 1), ("relay_b", 5), ("hop_b", 3), ("hop_a", 3), ("second", 2),
+    ("relay_a", 6), ("hop_a", 4), ("relay_b", 6), ("hop_b", 4), ("relay_z", 0),
+    ("relay_a", 7), ("relay_z", 1), ("hop_a", 5), ("hop_b", 5), ("relay_b", 7),
+    ("second", 3), ("hop_b", 6), ("hop_a", 6), ("second", 4), ("relay_z", 2),
+    ("hop_a", 7), ("hop_b", 7), ("second", 5), ("hop_h", 0), ("second", 6),
+    ("relay_z", 3), ("hop_h", 1), ("second", 7), ("finish", 0), ("hop_h", 2),
+    ("relay_z", 4), ("relay_z", 5), ("relay_z", 6), ("relay_z", 7), ("hop_h", 4),
+    ("hop_h", 3), ("hop_h", 5), ("finish", 6), ("finish", 1), ("finish", 3),
+    ("finish", 4), ("finish", 7), ("finish", 2), ("finish", 5),
 )
-ORDER_FIRST = 5
+ORDER_FIRST = 0
 
 
 def local(visibilities, col_offsets, row_offsets, facet_offsets, facet_order, vis_counts):
     vmem, smem = pltpu.VMEM, pltpu.SMEM
 
-    def twice(*shape):
-        return [vmem((NCH, *shape), BF16), vmem((NCH, *shape), BF16)]
+    def twice(*shape, chunks=NCH):
+        return [vmem((chunks, *shape), BF16), vmem((chunks, *shape), BF16)]
 
     scratch = [
         vmem((2, M, M), BF16),
-        vmem((NF, TR, 2 * M), BF16),
+        vmem((2, NF, TR, 2 * M), BF16),
+        vmem((CH, M), F32), vmem((CH, M), F32),
+        vmem((NF, M), F32), vmem((NF, M), F32),
         vmem((CH, M), F32), vmem((CH, M), F32),
         *twice(4, 2, TR, M),
         vmem((NCH, 4, 2, TR, M), F32),
@@ -351,10 +414,11 @@
         vmem((8, TR, 2 * M), BF16),
         vmem((2 * M, 2 * JB), BF16),
         vmem((NCH, 8, TR, 2 * JB), F32),
-        *twice(2, 3, TR, JB), *twice(4, TR, 2 * JB), *twice(TR, JB),
+        *twice(2, 3, TR, JB), *twice(4, TR, 2 * JB, chunks=len(NOT_MERGED)),
+        *twice(9, TR, JB, chunks=len(MERGED)), *twice(TR, JB, chunks=len(NOT_MERGED)),
         vmem((8, 128), F32), vmem((NF - 1, 8, 128), F32),
         pltpu.SemaphoreType.DMA,
-        pltpu.SemaphoreType.DMA((len(KINDS),)), pltpu.SemaphoreType.DMA((NCH, len(KINDS))),
+        pltpu.SemaphoreType.DMA((len(KINDS) + 1,)), pltpu.SemaphoreType.DMA((NCH, len(KINDS))),
         pltpu.SemaphoreType.DMA, pltpu.SemaphoreType.DMA,
     ]
     images, peak = pl.pallas_call(

time: 56.6 us -> 55.3 us (0.977)
  Pallas kernels: 53.3 us -> 52.1 us
    pallas_call x1, Pallas kernels: 53.3 us -> 52.1 us  [local(): pl.pallas_call(body, out_shape=(vmem((1, 2, FR, JB), F32), vmem((8, 128),...]
where the time goes in v5:
time: 55.3 us; the launch traced here: 55.2 us
  Pallas kernels  52.1 us (94%)
  between operations  1.93 us (3%)
  local copies, waits for them, and re-layouts  1.17 us (2%)
    pallas_call x1, Pallas kernels, local(): pl.pallas_call(body, out_shape=(vmem((1, 2, FR, JB), F32), vmem((8, 128),...  52.1 us

profile of v5, /device:TPU:8, one launch (start us, length us, event | category | flops | bytes accessed | tf_op | source)
XLA Modules:
  0.0 55.2 jit_solution(8108784471137543323)
XLA Ops:
  1.9 52.1 %image_step.1 = (f32[1,2,64,256]{3,2,1,0:T(8,128)S(1)}, f32[8,128]{1,0:T(8,128)S(1)}) custom-call(bf16[2,1024,1024]{2,1,0:T(8,128)(2,1)} %vis.1, s32[1]{0:T(128)S(6)} %copy.10.col_offsets, s32[16]{0:T(128)} %row_offsets.1, s32[2,16]{1,0:T(2,128)} %bitcast.2, s32[16]{0:T(128)} %facet_order.1, s32[1,1]{1,0:T(1,128)S(6)} %copy.11.vis_counts), custom_call_target="tpu_custom_call" | custom-call | tf_op jit(solution)/shard_map/image_step/pallas_call | solution.py:424
  54.0 0.5 slice.3
  54.5 0.7 %copy.9 = f32[1,2,64,256]{3,2,1,0:T(8,128)} copy(f32[1,2,64,256]{3,2,1,0:T(8,128)S(1)} %get-tuple-element.6) | data formatting | bytes 262144
